TPU v7x, 256 devices: a whole 4x4x8 slice. The times are simulated.
256 devices in a mesh: section: 8 (over x, core), fsdp: 32 (over y, z).
Axes of the slice: x: 4, y: 4, z: 8, core: 2. Of those that a mesh axis runs over, the one named last changes fastest.
Arguments:
- tokens: bfloat16 [8, 2, 4096, 8192], P('section', None, 'fsdp'), may hold values from -6 to 6
- queries: bfloat16 [8, 2, 4096, 4096], P('section', None, 'fsdp'), may hold values from -200 to 200
- gains: bfloat16 [8, 8192], P('section'), may hold values from 0.5 to 1.5
- key_weight: bfloat16 [8, 8192, 512], P('section', 'fsdp'), may hold values from -0.0625 to 0.0625
- value_weight: bfloat16 [8, 8192, 512], P('section', 'fsdp'), may hold values from -0.0625 to 0.0625
- lengths: int32 [2, 64], replicated, may hold values from 1 to 128, 4096 in all within a row
Outputs:
- attended: bfloat16 [8, 2, 4096, 4096], P('section', None, 'fsdp')
Inputs may be any that keep to these rules, and one draw needn't show every extreme that they name: `lengths`: each row sums to 4096; some document has exactly 128 tokens.
All inputs are finite; a program needn't handle non-finite values.
Results may differ from a plain program's by a relative error of at most 0.012.
The roundings to bfloat16 on the way count: a program that leaves them out, or rounds other values in their place, can miss the bound.
Values may be sent and summed in bfloat16 or wider, within the bound.
No kernel may reach another device: no remote copies, remote signals or barrier semaphores. Data moves between devices by JAX's collectives and lax.ppermute only.
A program may use at most 128 MiB of HBM per device.

v0:
```python
import jax
import jax.numpy as jnp
from jax import lax
from jax.sharding import PartitionSpec as P

HEAD = 128


def side_by_side(arrays, axis, dim, along):
    both = jnp.concatenate(arrays, axis=along)
    out, at, finished = (lax.all_gather(both, axis, axis=dim, tiled=True), 0, [])
    for a in arrays:
        finished.append(lax.slice_in_dim(out, at, at + a.shape[along], axis=along))
        at += a.shape[along]
    return tuple(finished)


def passed_along(block, axis, distance):
    devices = range(lax.axis_size(axis))
    route = [(i - distance, i) for i in devices if i - distance in devices]
    return lax.ppermute(block, axis, route)


def rms_norm(hidden, gain_row):
    widened = hidden.astype(jnp.float32)
    inverse_rms = lax.rsqrt(jnp.mean(widened * widened, axis=-1, keepdims=True) + 1e-05)
    return (widened * inverse_rms * gain_row.astype(jnp.float32)).astype(jnp.bfloat16)


def document_ids(length_row, positions):
    bounds = jnp.cumsum(length_row)
    return jnp.sum((bounds[None, :] <= positions[:, None]).astype(jnp.int32), axis=1)


def block_attend(query_rows, key_rows, value_rows, query_pos, key_pos, query_doc, key_doc):
    query_count = query_rows.shape[0]
    key_count = key_rows.shape[0]
    kv_count = key_rows.shape[1] // HEAD
    group_count = query_rows.shape[1] // (kv_count * HEAD)
    query_heads = query_rows.reshape(query_count, kv_count, group_count, HEAD)
    key_heads = key_rows.reshape(key_count, kv_count, HEAD)
    value_heads = value_rows.reshape(key_count, kv_count, HEAD)
    scores = jnp.einsum(
        "tkgd,skd->kgts", query_heads, key_heads, preferred_element_type=jnp.float32
    ) * HEAD ** (-0.5)
    allowed = (
        (key_doc[None, :] == query_doc[:, None])
        & (key_pos[None, :] <= query_pos[:, None])
        & (key_pos[None, :] >= 0)
    )
    scores = jnp.where(allowed, scores, -1e30)
    maxima = jnp.max(scores, axis=-1, keepdims=True)
    exponent = jnp.where(allowed, jnp.exp(scores - maxima), 0.0)
    totals = jnp.sum(exponent, axis=-1, keepdims=True)
    softmax_rows = (exponent / totals).astype(jnp.bfloat16)
    mixed = jnp.einsum(
        "kgts,skd->tkgd", softmax_rows, value_heads, preferred_element_type=jnp.float32
    )
    return mixed.reshape(query_count, kv_count * group_count * HEAD).astype(jnp.bfloat16)


def body(tokens, queries, gains, key_weight, value_weight, lengths):
    slot_count = tokens.shape[1]
    tok_count = tokens.shape[2]
    key_width = key_weight.shape[2]
    normed = rms_norm(tokens[0], gains[0])
    flat_rows = normed.reshape(slot_count * tok_count, normed.shape[2])

    def add_rows(weight_piece):
        return jnp.dot(flat_rows, weight_piece, preferred_element_type=jnp.float32)

    pieces = side_by_side((key_weight[0], value_weight[0]), "fsdp", 0, 1)
    key_sums = add_rows(pieces[0])
    value_sums = add_rows(pieces[1])
    own_keys = key_sums.astype(jnp.bfloat16).reshape(slot_count, tok_count, key_width)
    own_values = value_sums.astype(jnp.bfloat16).reshape(slot_count, tok_count, key_width)
    prior_keys, prior_values = passed_along((own_keys, own_values), "fsdp", 1)
    all_keys = jnp.concatenate([prior_keys, own_keys], axis=1)
    all_values = jnp.concatenate([prior_values, own_values], axis=1)
    fsdp_index = lax.axis_index("fsdp")
    query_pos = fsdp_index * tok_count + jnp.arange(tok_count, dtype=jnp.int32)
    key_pos = fsdp_index * tok_count - tok_count + jnp.arange(2 * tok_count, dtype=jnp.int32)
    outputs = []
    for slot_index in range(slot_count):
        outputs.append(
            block_attend(
                queries[0, slot_index],
                all_keys[slot_index],
                all_values[slot_index],
                query_pos,
                key_pos,
                document_ids(lengths[slot_index], query_pos),
                document_ids(lengths[slot_index], key_pos),
            )
        )
    return jnp.stack(outputs)[None]


def solution(mesh):
    return jax.shard_map(
        body,
        mesh=mesh,
        in_specs=(
            P("section", None, "fsdp", None),
            P("section", None, "fsdp", None),
            P("section", None),
            P("section", "fsdp", None),
            P("section", "fsdp", None),
            P(),
        ),
        out_specs=P("section", None, "fsdp", None),
        check_vma=False,
    )
```

profile of v0, /device:TPU:8, one launch (start us, length us, event | category | flops | bytes accessed | tf_op | source)
XLA Modules:
  0.0 202.2 jit_solution(9059581040976685564)
XLA Ops:
  6.5 0.0 all-gather.2.cloned.1.call-start
  6.5 1.9 pad_maximum_fusion
  8.4 0.0 all-gather.2.cloned.1.call-update
  8.4 0.8 convert_element_type.101
  9.2 0.8 slice_bitcast_fusion
  10.0 0.1 copy.32
  10.1 0.1 reduce-window.16
  10.2 0.1 reduce.1
  10.3 0.1 copy.40
  10.4 0.1 reduce-window.17
  10.5 0.1 reduce.2
  10.6 1.7 fusion.38
  12.3 0.7 copy.60
  13.0 0.7 copy.59
  13.6 0.0 copy-start
  13.7 0.1 convert_reduce_fusion.3
  13.8 0.1 convert_reduce_fusion.1
  13.9 3.3 %multiply_reduce_fusion = f32[2,128]{1,0:T(2,128)S(1)} fusion(bf16[1,2,128,8192]{3,2,1,0:T(8,128)(2,1)} %param.6), kind=kLoop, calls=%fused_computation.9 | loop fusion | flops 6291200 | bytes 4195328 | tf_op jit(solution)/shard_map/reduce_sum | solution.py:26
  17.2 0.0 copy-done
  17.2 3.1 %fusion.7 = bf16[256,8192]{1,0:T(8,128)(2,1)} fusion(f32[8192]{0:T(1024)S(1)} %bitcast.94, f32[256]{0:T(256)S(1)} %rsqrt_bitcast_fusion, bf16[1,2,128,8192]{3,2,1,0:T(8,128)(2,1)S(1)} %copy-done), kind=kLoop, calls=%fused_computation.8 | loop fusion | flops 8388608 | bytes 8422400 | tf_op jit(solution)/shard_map/convert_element_type | solution.py:27
  20.3 131.0 %all-gather.2.cloned.1.call-done = bf16[8192,1024]{1,0:T(8,128)(2,1)} async-done(((bf16[256,1024]{1,0:T(8,128)(2,1)}), bf16[8192,1024]{1,0:T(8,128)(2,1)}) %all-gather.2.cloned.1.call-update) | async-done | bytes 16777232 | tf_op jit(solution)/shard_map/all_gather | solution.py:11
  151.3 0.0 copy-start.1
  151.3 7.1 %fusion.20 = bf16[256,512]{1,0:T(8,128)(2,1)S(1)} fusion(bf16[256,8192]{1,0:T(8,128)(2,1)} %fusion.7, bf16[8192,1024]{1,0:T(8,128)(2,1)} %all-gather.2.cloned.1.call-done), kind=kOutput, calls=%fused_computation.29 | convolution fusion | flops 2147614720 | bytes 12845056 | tf_op jit(solution)/shard_map/dot_general | solution.py:70
  158.4 1.9 collective-permute-start
  160.3 0.0 copy-done.1
  160.4 5.7 %fusion.23 = bf16[256,512]{1,0:T(8,128)(2,1)S(1)} fusion(bf16[256,8192]{1,0:T(8,128)(2,1)S(1)} %copy-done.1, bf16[8192,1024]{1,0:T(8,128)(2,1)} %all-gather.2.cloned.1.call-done), kind=kOutput, calls=%fused_computation.30 | convolution fusion | flops 2147614720 | bytes 12845056 | tf_op jit(solution)/shard_map/dot_general | solution.py:70
  166.1 0.2 copy.33
  166.3 3.2 %collective-permute-start.1 = (bf16[2,128,512]{1,2,0:T(8,128)(2,1)S(1)}, bf16[2,128,512]{1,2,0:T(8,128)(2,1)S(1)}, u32[]{:S(2)}, u32[]{:S(2)}) collective-permute-start(bf16[2,128,512]{1,2,0:T(8,128)(2,1)S(1)} %copy.33), channel_id=1, source_target_pairs={{0,1},{1,2},{2,3},{3,4},{4,5},{5,6},{6,7},{7,8},{8,9},{9,10},{10,1... | collective-permute-start | bytes 786440 | tf_op jit(solution)/shard_map/ppermute | solution.py:21
  169.5 0.2 fusion.32
  169.7 0.1 collective-permute-done
  169.8 1.0 fusion.31
  170.8 0.1 copy.39
  171.0 6.6 %collective-permute-done.1 = bf16[2,128,512]{1,2,0:T(8,128)(2,1)S(1)} collective-permute-done((bf16[2,128,512]{1,2,0:T(8,128)(2,1)S(1)}, bf16[2,128,512]{1,2,0:T(8,128)(2,1)S(1)}, u32[]{:S(2)}, u32[]{:S(2)}) %collective-permute-start.1) | collective-permute-done | bytes 262176 | tf_op jit(solution)/shard_map/ppermute | solution.py:21
  177.6 0.8 fusion.30
  178.4 3.6 %fusion.39 = (f32[4,8,128]{2,1,0:T(8,128)S(1)}, f32[4,8,128,256]{2,3,1,0:T(8,128)}) fusion(pred[128,256]{0,1:T(8,128)(4,1)S(1)} %get-tuple-element.16, bf16[256,4,128,1]{0,2,3,1:T(8,128)(2,1)S(1)} %bitcast.93, bf16[128,4,8,128]{0,3,2,1:T(8,128)(2,1)S(1)} %bitcast.82), kind=kOutput, calls=%fused_computation.61 | convolution fusion | flops 273678592 | bytes 5554176 | tf_op jit(solution)/shard_map/sub | solution.py:53
  182.0 2.7 %fusion.18 = bf16[4,128,8,128]{3,1,2,0:T(8,128)(2,1)S(1)} fusion(bf16[256,4,128,1]{0,2,3,1:T(8,128)(2,1)S(1)} %bitcast.85, f32[4,8,128,256]{2,3,1,0:T(8,128)} %get-tuple-element.20, f32[4,8,128]{2,1,0:T(8,128)S(1)} %get-tuple-element.19), kind=kOutput, calls=%fused_computation.27 | convolution fusion | flops 271056896 | bytes 5521408 | tf_op jit(solution)/shard_map/kgts,skd->tkgd/dot_general | solution.py:56
  184.7 0.5 copy.46
  185.2 0.8 copy.31
  186.0 0.0 copy-start.2
  186.0 4.6 %fusion.40 = (f32[4,8,128]{2,1,0:T(8,128)S(1)}, f32[4,8,128,256]{2,3,1,0:T(8,128)}) fusion(pred[128,256]{0,1:T(8,128)(4,1)S(1)} %get-tuple-element.15, bf16[256,4,128,1]{0,2,3,1:T(8,128)(2,1)} %bitcast.92, bf16[128,4,8,128]{0,3,2,1:T(8,128)(2,1)S(1)} %bitcast.81), kind=kOutput, calls=%fused_computation.62 | convolution fusion | flops 273678592 | bytes 5554176 | tf_op jit(solution)/shard_map/sub | solution.py:53
  190.6 0.0 copy-done.2
  190.6 2.7 %fusion.19 = bf16[4,128,8,128]{3,1,2,0:T(8,128)(2,1)S(1)} fusion(bf16[256,4,128,1]{0,2,3,1:T(8,128)(2,1)S(1)} %bitcast.86, f32[4,8,128,256]{2,3,1,0:T(8,128)} %get-tuple-element.22, f32[4,8,128]{2,1,0:T(8,128)S(1)} %get-tuple-element.21), kind=kOutput, calls=%fused_computation.28 | convolution fusion | flops 271056896 | bytes 5521408 | tf_op jit(solution)/shard_map/kgts,skd->tkgd/dot_general | solution.py:56
  193.3 0.5 copy.45
  193.9 1.5 maximum_bitcast_fusion
  (4 shorter events, 0.0 us)
Async XLA Ops:
  6.5 144.8 %all-gather.2.cloned.1.call-start = ((), (), s32[]{:S(2)}) async-start(), calls=%async_computation | async-start | bytes 17301504 | tf_op jit(solution)/shard_map/all_gather | solution.py:11
  13.6 3.5 %copy-start = (bf16[1,2,128,8192]{3,2,1,0:T(8,128)(2,1)S(1)}, bf16[1,2,128,8192]{3,2,1,0:T(8,128)(2,1)}, u32[]{:S(2)}) copy-start(bf16[1,2,128,8192]{3,2,1,0:T(8,128)(2,1)} %param.6) | copy-start | bytes 12582916
  151.3 9.1 %copy-start.1 = (bf16[256,8192]{1,0:T(8,128)(2,1)S(1)}, bf16[256,8192]{1,0:T(8,128)(2,1)}, u32[]{:S(2)}) copy-start(bf16[256,8192]{1,0:T(8,128)(2,1)} %fusion.7) | copy-start | bytes 12582916
  158.4 11.4 %collective-permute-start = (bf16[2,128,512]{2,1,0:T(8,128)(2,1)S(1)}, bf16[2,128,512]{2,1,0:T(8,128)(2,1)}, u32[]{:S(2)}, u32[]{:S(2)}) collective-permute-start(bf16[2,128,512]{2,1,0:T(8,128)(2,1)S(1)} %bitcast.90), channel_id=1, source_target_pairs={{0,1},{1,2},{2,3},{3,4},{4,5},{5,6},{6,7},{7,8},{8,9},{9,10},{10,1... | collective-permute-start | bytes 786440 | tf_op jit(solution)/shard_map/ppermute | solution.py:21
  166.3 11.3 %collective-permute-start.1 = (bf16[2,128,512]{1,2,0:T(8,128)(2,1)S(1)}, bf16[2,128,512]{1,2,0:T(8,128)(2,1)S(1)}, u32[]{:S(2)}, u32[]{:S(2)}) collective-permute-start(bf16[2,128,512]{1,2,0:T(8,128)(2,1)S(1)} %copy.33), channel_id=1, source_target_pairs={{0,1},{1,2},{2,3},{3,4},{4,5},{5,6},{6,7},{7,8},{8,9},{9,10},{10,1... | collective-permute-start | bytes 786440 | tf_op jit(solution)/shard_map/ppermute | solution.py:21
  186.0 4.6 %copy-start.2 = (bf16[1,256,512]{1,2,0:T(8,128)(2,1)S(1)}, bf16[1,256,512]{1,2,0:T(8,128)(2,1)}, u32[]{:S(2)}) copy-start(bf16[1,256,512]{1,2,0:T(8,128)(2,1)} %copy.31) | copy-start | bytes 786436
Sparse Core Ops, SparseCore 0:
  9.9 141.3 all-gather.1
where the time goes:
time: 203 us; the launch traced here: 202 us
  waiting for transfers between devices  138 us (68%)
  matrix products  26.4 us (13%)
  between operations  13.6 us (7%)
  other arithmetic  13.1 us (6%)
  local copies, waits for them, and re-layouts  6.17 us (3%)
  starting transfers between devices  5.17 us (3%)
    all_gather x1, waiting for transfers between devices, side_by_side(): lax.all_gather(both, axis, axis=dim, tiled=True)  131 us
    dot_general x2, matrix products, add_rows(): return jnp.dot(flat_rows, weight_piece, preferred_element_type=jnp.float32)  12.9 us
    sub x2, matrix products, block_attend(): exponent = jnp.where(allowed, jnp.exp(scores - maxima), 0.0)  8.17 us
    ppermute x2, waiting for transfers between devices, passed_along(): return lax.ppermute(block, axis, route)  6.72 us
    dot_general x2, matrix products, block_attend(): jnp.einsum('kgts,skd->tkgd', softmax_rows, value_heads, preferred_element...  5.4 us
    ppermute x2, starting transfers between devices, passed_along(): return lax.ppermute(block, axis, route)  5.16 us
  transfers between devices with their start and end apart: 3, of which 3 were waited for; matrix products, arithmetic and copies ran while one was open for 9% of the time, Pallas kernels for 0%

commit v1 on v0

v1 whole, which is shorter than its diff:
```python
import jax
import jax.numpy as jnp
from jax import lax
from jax.experimental import pallas as pl
from jax.experimental.pallas import tpu as pltpu
from jax.sharding import Mesh, PartitionSpec as P


HEAD = 128
Y, Z = 4, 8


def cost(flops, nbytes):
    return pl.CostEstimate(flops=flops, bytes_accessed=nbytes, transcendentals=0)


def vmem():
    return pl.BlockSpec(memory_space=pltpu.VMEM)


def any_space():
    return pl.BlockSpec(memory_space=pl.ANY)


def norm_kernel(y_ref, x_ref, g_ref, *out_refs):
    x = x_ref[...].astype(jnp.float32)
    inv = lax.rsqrt(jnp.mean(x * x, axis=-1, keepdims=True) + 1e-05)
    width = x_ref.shape[1] // Y
    for j in range(Y):
        at = pl.multiple_of(((y_ref[0] + j) % Y) * width, width)
        cols = x_ref[:, pl.ds(at, width)].astype(jnp.float32)
        gain = g_ref[:, pl.ds(at, width)].astype(jnp.float32)
        out_refs[j][...] = (cols * inv * gain).astype(jnp.bfloat16)


def norm_quarters(rows, gain, y_index):
    count, width = rows.shape
    step = 32
    return pl.pallas_call(
        norm_kernel,
        grid_spec=pltpu.PrefetchScalarGridSpec(
            num_scalar_prefetch=1,
            grid=(count // step,),
            in_specs=[
                pl.BlockSpec((step, width), lambda i, y: (i, 0)),
                pl.BlockSpec((1, width), lambda i, y: (0, 0)),
            ],
            out_specs=[pl.BlockSpec((step, width // Y), lambda i, y: (i, 0))] * Y,
        ),
        out_shape=[jax.ShapeDtypeStruct((count, width // Y), jnp.bfloat16)] * Y,
        cost_estimate=cost(20_000_000, 8 << 20),
        name="norm",
    )(y_index, rows, gain)


def product_kernel(slot_ref, *refs):
    a_refs, w_refs, refs = refs[:Y], refs[Y : Y + Z], refs[Y + Z :]
    own_refs, send_refs = refs[:2], refs[2:8]
    a_buf, wk, wv, a_sem, w_sem = refs[8:]
    deep = wk.shape[0] // Z
    copies = []
    for j in range(Z):
        at = pl.multiple_of(slot_ref[j] * deep, deep)
        for h, buf in enumerate((wk, wv)):
            c = pltpu.make_async_copy(w_refs[j].at[h], buf.at[pl.ds(at, deep)], w_sem.at[2 * j + h])
            c.start()
            copies.append(c)
    loads = [pltpu.make_async_copy(a_refs[j], a_buf.at[j], a_sem.at[j]) for j in range(Y)]
    for c in loads:
        c.start()
    for c in copies:
        c.wait()
    wide = wk.shape[1]
    half = a_buf.shape[1] // 2
    for j in range(Y):
        loads[j].wait()
        k = jnp.dot(a_buf[j], wk[...], preferred_element_type=jnp.float32)
        v = jnp.dot(a_buf[j], wv[...], preferred_element_type=jnp.float32)
        for m in range(2):
            km, vm = k[m * half : (m + 1) * half], v[m * half : (m + 1) * half]
            if j == 0:
                own_refs[m][:, :wide] = km
                own_refs[m][:, wide:] = vm
            else:
                high = km.astype(jnp.bfloat16)
                out = send_refs[3 * m + j - 1]
                out[:, :wide] = high
                out[:, wide : 2 * wide] = (km - high.astype(jnp.float32)).astype(jnp.bfloat16)
                out[:, 2 * wide :] = vm.astype(jnp.bfloat16)


def products(slots, acts, weights):
    rows, deep = acts[0].shape
    wide = weights[0].shape[2]
    half = rows // 2
    own = jax.ShapeDtypeStruct((half, 2 * wide), jnp.float32)
    send = jax.ShapeDtypeStruct((half, 3 * wide), jnp.bfloat16)
    return pl.pallas_call(
        product_kernel,
        in_specs=[pl.BlockSpec(memory_space=pltpu.SMEM)] + [any_space()] * (Y + Z),
        out_specs=[vmem()] * 8,
        out_shape=[own] * 2 + [send] * 6,
        scratch_shapes=[
            pltpu.VMEM((Y, rows, deep), jnp.bfloat16),
            pltpu.VMEM((deep, wide), jnp.bfloat16),
            pltpu.VMEM((deep, wide), jnp.bfloat16),
            pltpu.SemaphoreType.DMA((Y,)),
            pltpu.SemaphoreType.DMA((2 * Z,)),
        ],
        cost_estimate=cost(4 * Y * rows * deep * wide, 12 << 20),
        compiler_params=pltpu.CompilerParams(vmem_limit_bytes=40 << 20),
        name="products",
    )(slots, *acts, *weights)


def total_kernel(own_ref, *refs):
    parts, out_ref = refs[:3], refs[3]
    wide = own_ref.shape[1] // 2
    k, v = own_ref[:, :wide], own_ref[:, wide:]
    for p in parts:
        k = k + (p[:, :wide].astype(jnp.float32) + p[:, wide : 2 * wide].astype(jnp.float32))
        v = v + p[:, 2 * wide :].astype(jnp.float32)
    out_ref[:, :wide] = k.astype(jnp.bfloat16)
    out_ref[:, wide:] = v.astype(jnp.bfloat16)


def totals(own, parts):
    return pl.pallas_call(
        total_kernel,
        in_specs=[vmem()] * 4,
        out_specs=vmem(),
        out_shape=jax.ShapeDtypeStruct(own.shape, jnp.bfloat16),
        cost_estimate=cost(2_000_000, 2 << 20),
        name="totals",
    )(own, *parts)


def attend_kernel(first_ref, q_ref, pk_ref, k_ref, pv_ref, v_ref, *rest):
    out_ref = rest[-1]
    count = q_ref.shape[1]
    keys = jnp.concatenate([pk_ref[...], k_ref[...]], axis=0)
    values = jnp.concatenate([pv_ref[...], v_ref[...]], axis=0)
    column = lax.broadcasted_iota(jnp.int32, (count, 2 * count), 1)
    row = lax.broadcasted_iota(jnp.int32, (count, 2 * count), 0)
    allowed = (column >= first_ref[...]) & (column <= row + count)
    for g in range(q_ref.shape[2] // HEAD):
        q = q_ref[0, :, g * HEAD : (g + 1) * HEAD]
        s = lax.dot_general(q, keys, (((1,), (1,)), ((), ())), preferred_element_type=jnp.float32)
        s = jnp.where(allowed, s * HEAD ** (-0.5), -1e30)
        e = jnp.exp(s - jnp.max(s, axis=-1, keepdims=True))
        total = jnp.sum(e, axis=-1, keepdims=True)
        o = jnp.dot(e.astype(jnp.bfloat16), values, preferred_element_type=jnp.float32)
        out_ref[0, :, g * HEAD : (g + 1) * HEAD] = (o / total).astype(jnp.bfloat16)


def attend(slot, first, queries, prior, own, so_far):
    count, width = queries.shape[1], queries.shape[2]
    heads = own.shape[1] // (2 * HEAD)
    group = width // heads
    q_spec = pl.BlockSpec((1, count, group), lambda h: (slot, 0, h))
    k_spec = pl.BlockSpec((count, HEAD), lambda h: (0, h))
    v_spec = pl.BlockSpec((count, HEAD), lambda h: (0, h + heads))
    extra = [] if so_far is None else [so_far]
    return pl.pallas_call(
        attend_kernel,
        grid=(heads,),
        in_specs=[pl.BlockSpec((count, 1), lambda h: (0, 0)), q_spec, k_spec, k_spec, v_spec, v_spec]
        + [any_space()] * len(extra),
        out_specs=q_spec,
        out_shape=jax.ShapeDtypeStruct(queries.shape, jnp.bfloat16),
        input_output_aliases={6: 0} if extra else {},
        cost_estimate=cost(8 * count * count * width, 4 << 20),
        name="attend",
    )(first, queries, prior, own, prior, own, *extra)


def hop(block, axis, count, distance):
    return lax.ppermute(block, axis, [(i, (i + distance) % count) for i in range(count)])


def body(tokens, queries, gains, key_weight, value_weight, lengths):
    slots, count, width = tokens.shape[1:]
    y, z = lax.axis_index("y"), lax.axis_index("z")

    own_w = jnp.concatenate([key_weight, value_weight], axis=0)
    shards = [own_w]
    up = down = own_w
    ups, downs = [], []
    for _ in range(Z // 2 - 1):
        up = hop(up, "z", Z, 1)
        down = hop(down, "z", Z, -1)
        ups.append(up)
        downs.append(down)
    far_k = hop(up[:1], "z", Z, 1)
    far_v = hop(down[1:], "z", Z, -1)
    far = jnp.concatenate([far_k, far_v], axis=0)
    shards = [own_w] + ups + downs + [far]
    offsets = [0] + [s + 1 for s in range(Z // 2 - 1)] + [-s - 1 for s in range(Z // 2 - 1)] + [Z // 2]
    places = (z - jnp.array(offsets, jnp.int32)) % Z

    quarters = norm_quarters(
        tokens[0].reshape(slots * count, width), gains, y.reshape(1).astype(jnp.int32)
    )
    acts = [quarters[0]]
    for j in range(1, Y):
        acts.append(hop(quarters[j], "y", Y, j))

    pieces = products(places, acts, shards)
    own_parts, sends = pieces[:2], pieces[2:]

    bounds = jnp.sum(
        jnp.where(
            jnp.arange(lengths.shape[1])[None, :, None] <= jnp.arange(lengths.shape[1])[None, None, :],
            lengths[:, :, None],
            0,
        ),
        axis=1,
    )
    base = (y * Z + z) * count
    position = base + jnp.arange(count, dtype=jnp.int32)
    first = jnp.max(
        jnp.where(bounds[:, None, :] <= position[None, :, None], bounds[:, None, :], 0),
        axis=2,
        keepdims=True,
    )
    first = first - (base - count)

    back = []
    for m in range(slots):
        got = []
        for j in range(1, Y):
            got.append(hop(sends[3 * m + j - 1], "y", Y, -j))
        back.append(got)
    out = None
    for m in range(slots):
        own = totals(own_parts[m], back[m])
        prior = hop(own, ("y", "z"), Y * Z, 1)
        out = attend(m, first[m], queries[0], prior, own, out)
    return out[None]


def solution(mesh):
    split = Mesh(mesh.devices.reshape(-1, Y, Z), ("section", "y", "z"))
    spread = ("y", "z")

    return jax.shard_map(
        body,
        mesh=split,
        in_specs=(
            P("section", None, spread, None),
            P("section", None, spread, None),
            P("section", None),
            P("section", spread, None),
            P("section", spread, None),
            P(),
        ),
        out_specs=P("section", None, spread, None),
        check_vma=False,
    )
```

time: 203 us -> 158 us (0.78)
  the two profiles are of different devices: /device:TPU:8 before, /device:TPU:4 now
where the time goes in v1:
time: 158 us; the launch traced here: 157 us
  waiting for transfers between devices  83.3 us (53%)
  starting transfers between devices  30.8 us (19%)
  Pallas kernels  30.4 us (19%)
  local copies, waits for them, and re-layouts  11.2 us (7%)
    ppermute x19, waiting for transfers between devices, hop(): lax.ppermute(block, axis, [(i, (i + distance) % count) for i in range(cou...  83.3 us
    ppermute x19, starting transfers between devices, hop(): lax.ppermute(block, axis, [(i, (i + distance) % count) for i in range(cou...  30.8 us
    pallas_call x2, Pallas kernels, attend(): pl.pallas_call(attend_kernel, grid=(heads,), in_specs=[pl.BlockSpec((coun...  10.8 us
    unnamed x35, local copies, waits for them, and re-layouts  8.02 us
    pallas_call x1, Pallas kernels, products(): pl.pallas_call(product_kernel, in_specs=[pl.BlockSpec(memory_space=pltpu....  7.73 us
    pallas_call x1, Pallas kernels, norm_quarters(): pl.pallas_call(norm_kernel, grid_spec=pltpu.PrefetchScalarGridSpec(num_sc...  7.36 us
    pallas_call x2, Pallas kernels, totals(): pl.pallas_call(total_kernel, in_specs=[vmem()] * 4, out_specs=vmem(), out...  4.52 us
  transfers between devices with their start and end apart: 19, of which 11 were waited for; matrix products, arithmetic and copies ran while one was open for 2% of the time, Pallas kernels for 11%

profile of v1, /device:TPU:4, one launch (start us, length us, event | category | flops | bytes accessed | tf_op | source)
XLA Modules:
  0.0 157.2 jit_solution(13117906328210087209)
XLA Ops:
  0.0 1.0 constant_dynamic-update-slice_fusion.1
  1.0 1.0 constant_dynamic-update-slice_fusion.refs_4_
  1.9 5.9 %collective-permute-start.6 = (bf16[2,256,512]{2,1,0:T(8,128)(2,1)S(1)}, bf16[2,256,512]{2,1,0:T(8,128)(2,1)S(1)}, u32[]{:S(2)}, u32[]{:S(2)}) collective-permute-start(bf16[2,256,512]{2,1,0:T(8,128)(2,1)S(1)} %constant_dynamic-update-slice_fusion.refs_4_), channel_id=1, source_target_pairs={{0,7},{1,0},{2,1},{3,2},{4,3},{5,4},{6,5},{7,6},{8,15},{9,8},{10,9... | collective-permute-start | bytes 1572872 | tf_op jit(solution)/shard_map/ppermute | solution.py:178
  7.9 0.0 collective-permute-start.3
  7.9 11.2 %collective-permute-done.6.refs_8_ = bf16[2,256,512]{2,1,0:T(8,128)(2,1)S(1)} collective-permute-done((bf16[2,256,512]{2,1,0:T(8,128)(2,1)S(1)}, bf16[2,256,512]{2,1,0:T(8,128)(2,1)S(1)}, u32[]{:S(2)}, u32[]{:S(2)}) %collective-permute-start.6) | collective-permute-done | bytes 524320 | tf_op jit(solution)/shard_map/ppermute | solution.py:178
  19.1 3.7 %collective-permute-start.7 = (bf16[2,256,512]{2,1,0:T(8,128)(2,1)S(1)}, bf16[2,256,512]{2,1,0:T(8,128)(2,1)}, u32[]{:S(2)}, u32[]{:S(2)}) collective-permute-start(bf16[2,256,512]{2,1,0:T(8,128)(2,1)S(1)} %collective-permute-done.6.refs_8_), channel_id=1, source_target_pairs={{0,7},{1,0},{2,1},{3,2},{4,3},{5,4},{6,5},{7,6},{8,15},{9,8},{10,9... | collective-permute-start | bytes 1572872 | tf_op jit(solution)/shard_map/ppermute | solution.py:178
  22.8 0.0 collective-permute-done.3.refs_5_
  22.8 0.0 collective-permute-start.4
  22.8 0.0 copy-start.16
  22.8 7.4 %norm.1 = (bf16[256,2048]{1,0:T(8,128)(2,1)}, bf16[256,2048]{1,0:T(8,128)(2,1)}, bf16[256,2048]{1,0:T(8,128)(2,1)}, bf16[256,2048]{1,0:T(8,128)(2,1)}) custom-call(s32[1]{0:T(128)} %bitcast.2.y_ref, bf16[256,8192]{1,0:T(8,128)(2,1)} %bitcast.10, bf16[1,8192]{1,0:T(2,128)(2,1)} %g_ref.1), custom_call_target="tpu_custom_call" | custom-call | flops 20000000 | bytes 8388608 | tf_op jit(solution)/shard_map/norm/pallas_call | solution.py:39
  30.1 0.0 copy-done.3
  30.1 1.7 %collective-permute-start = (bf16[256,2048]{1,0:T(8,128)(2,1)}, bf16[256,2048]{1,0:T(8,128)(2,1)}, u32[]{:S(2)}, u32[]{:S(2)}) collective-permute-start(bf16[256,2048]{1,0:T(8,128)(2,1)} %get-tuple-element.18), channel_id=1, source_target_pairs={{0,8},{8,16},{16,24},{24,0},{1,9},{9,17},{17,25},{25,1},{2,10},{10... | collective-permute-start | bytes 3145736 | tf_op jit(solution)/shard_map/ppermute | solution.py:178
  31.8 2.9 %collective-permute-start.1 = (bf16[256,2048]{1,0:T(8,128)(2,1)}, bf16[256,2048]{1,0:T(8,128)(2,1)}, u32[]{:S(2)}, u32[]{:S(2)}) collective-permute-start(bf16[256,2048]{1,0:T(8,128)(2,1)} %get-tuple-element.19), channel_id=1, source_target_pairs={{0,16},{8,24},{16,0},{24,8},{1,17},{9,25},{17,1},{25,9},{2,18},{10... | collective-permute-start | bytes 3145736 | tf_op jit(solution)/shard_map/ppermute | solution.py:178
  34.7 1.3 collective-permute-start.2
  36.1 0.0 collective-permute-done.7.refs_9_
  36.1 3.0 %collective-permute-start.8 = (bf16[2,256,512]{2,1,0:T(8,128)(2,1)}, bf16[2,256,512]{2,1,0:T(8,128)(2,1)S(1)}, u32[]{:S(2)}, u32[]{:S(2)}) collective-permute-start(bf16[2,256,512]{2,1,0:T(8,128)(2,1)} %collective-permute-done.7.refs_9_), channel_id=1, source_target_pairs={{0,7},{1,0},{2,1},{3,2},{4,3},{5,4},{6,5},{7,6},{8,15},{9,8},{10,9... | collective-permute-start | bytes 1572872 | tf_op jit(solution)/shard_map/ppermute | solution.py:178
  39.1 0.0 collective-permute-done.4.refs_6_
  39.1 0.0 collective-permute-start.5
  39.1 9.2 %collective-permute-done.8.refs_10_ = bf16[2,256,512]{2,1,0:T(8,128)(2,1)S(1)} collective-permute-done((bf16[2,256,512]{2,1,0:T(8,128)(2,1)}, bf16[2,256,512]{2,1,0:T(8,128)(2,1)S(1)}, u32[]{:S(2)}, u32[]{:S(2)}) %collective-permute-start.8) | collective-permute-done | bytes 524320 | tf_op jit(solution)/shard_map/ppermute | solution.py:178
  48.4 3.7 %collective-permute-start.10 = (bf16[1,256,512]{2,1,0:T(8,128)(2,1)S(1)}, bf16[1,256,512]{2,1,0:T(8,128)(2,1)}, u32[]{:S(2)}, u32[]{:S(2)}) collective-permute-start(bf16[1,256,512]{2,1,0:T(8,128)(2,1)S(1)} %slice.19), channel_id=1, source_target_pairs={{0,7},{1,0},{2,1},{3,2},{4,3},{5,4},{6,5},{7,6},{8,15},{9,8},{10,9... | collective-permute-start | bytes 786440 | tf_op jit(solution)/shard_map/ppermute | solution.py:178
  52.0 0.0 collective-permute-done.5.refs_7_
  52.0 0.7 slice.18
  52.8 0.0 collective-permute-start.9
  52.8 3.1 %collective-permute-done.10 = bf16[1,256,512]{2,1,0:T(8,128)(2,1)} collective-permute-done((bf16[1,256,512]{2,1,0:T(8,128)(2,1)S(1)}, bf16[1,256,512]{2,1,0:T(8,128)(2,1)}, u32[]{:S(2)}, u32[]{:S(2)}) %collective-permute-start.10) | collective-permute-done | bytes 262176 | tf_op jit(solution)/shard_map/ppermute | solution.py:178
  55.9 4.7 %collective-permute-done.9 = bf16[1,256,512]{2,1,0:T(8,128)(2,1)} collective-permute-done((bf16[1,256,512]{2,1,0:T(8,128)(2,1)}, bf16[1,256,512]{2,1,0:T(8,128)(2,1)}, u32[]{:S(2)}, u32[]{:S(2)}) %collective-permute-start.9) | collective-permute-done | bytes 262176 | tf_op jit(solution)/shard_map/ppermute | solution.py:178
  60.7 1.1 pad_maximum_fusion.refs_11_
  61.7 0.0 collective-permute-done.refs_1_
  61.7 17.5 %collective-permute-done.1.refs_2_ = bf16[256,2048]{1,0:T(8,128)(2,1)} collective-permute-done((bf16[256,2048]{1,0:T(8,128)(2,1)}, bf16[256,2048]{1,0:T(8,128)(2,1)}, u32[]{:S(2)}, u32[]{:S(2)}) %collective-permute-start.1) | collective-permute-done | bytes 1048608 | tf_op jit(solution)/shard_map/ppermute | solution.py:178
  79.2 0.0 collective-permute-done.2.refs_3_
  79.2 1.0 copy-done.4
  80.3 7.7 %products.1 = (f32[128,1024]{1,0:T(8,128)S(1)}, f32[128,1024]{1,0:T(8,128)S(1)}, bf16[128,1536]{1,0:T(8,128)(2,1)}, bf16[128,1536]{1,0:T(8,128)(2,1)}, bf16[128,...) custom-call(s32[8]{0:T(128)S(1)} %and_select_fusion.slot_ref, ...), custom_call_target="tpu_custom_call" | custom-call | flops 4294967296 | bytes 12582912 | tf_op jit(solution)/shard_map/products/pallas_call | solution.py:98
  88.0 0.0 copy-start
  88.0 0.8 copy-done
  88.8 0.8 copy-done.1
  89.6 0.8 copy-done.5
  90.4 0.7 copy-done.6
  91.1 2.2 %collective-permute-start.15 = (bf16[128,1536]{1,0:T(8,128)(2,1)}, bf16[128,1536]{1,0:T(8,128)(2,1)S(1)}, u32[]{:S(2)}, u32[]{:S(2)}) collective-permute-start(bf16[128,1536]{1,0:T(8,128)(2,1)} %get-tuple-element.26), channel_id=1, source_target_pairs={{0,24},{8,0},{16,8},{24,16},{1,25},{9,1},{17,9},{25,17},{2,26},{10... | collective-permute-start | bytes 1179656 | tf_op jit(solution)/shard_map/ppermute | solution.py:178
  93.3 1.1 collective-permute-start.16
  94.4 0.7 collective-permute-start.17
  95.1 0.1 select_reduce_fusion.1
  95.2 2.6 %collective-permute-start.11 = (bf16[128,1536]{1,0:T(8,128)(2,1)}, bf16[128,1536]{1,0:T(8,128)(2,1)S(1)}, u32[]{:S(2)}, u32[]{:S(2)}) collective-permute-start(bf16[128,1536]{1,0:T(8,128)(2,1)} %copy-done.6), channel_id=1, source_target_pairs={{0,24},{8,0},{16,8},{24,16},{1,25},{9,1},{17,9},{25,17},{2,26},{10... | collective-permute-start | bytes 1179656 | tf_op jit(solution)/shard_map/ppermute | solution.py:178
  97.9 1.2 collective-permute-start.12
  99.0 12.3 %collective-permute-done.15.refs_0_ = bf16[128,1536]{1,0:T(8,128)(2,1)S(1)} collective-permute-done((bf16[128,1536]{1,0:T(8,128)(2,1)}, bf16[128,1536]{1,0:T(8,128)(2,1)S(1)}, u32[]{:S(2)}, u32[]{:S(2)}) %collective-permute-start.15) | collective-permute-done | bytes 393248 | tf_op jit(solution)/shard_map/ppermute | solution.py:178
  111.4 0.8 collective-permute-start.13
  112.2 0.1 select_reduce_fusion
  112.3 0.0 collective-permute-done.16.refs_1_
  112.3 3.2 %collective-permute-done.17.refs_2_ = bf16[128,1536]{1,0:T(8,128)(2,1)S(1)} collective-permute-done((bf16[128,1536]{1,0:T(8,128)(2,1)}, bf16[128,1536]{1,0:T(8,128)(2,1)S(1)}, u32[]{:S(2)}, u32[]{:S(2)}) %collective-permute-start.17) | collective-permute-done | bytes 393248 | tf_op jit(solution)/shard_map/ppermute | solution.py:178
  115.5 0.7 copy-done.13
  116.2 2.3 %totals.3.k_ref.v_ref = bf16[128,1024]{1,0:T(8,128)(2,1)} custom-call(f32[128,1024]{1,0:T(8,128)} %copy-done.1, bf16[128,1536]{1,0:T(8,128)(2,1)} %copy-done.10, bf16[128,1536]{1,0:T(8,128)(2,1)} %copy-done.12, bf16[128,1536]{1,0:T(8,128)(2,1)} %copy-done.13), custom_call_target="tpu_custom_call" | custom-call | flops 2000000 | bytes 2097152 | tf_op jit(solution)/shard_map/totals/pallas_call | solution.py:128
  118.5 0.0 collective-permute-start.18
  118.5 8.9 %collective-permute-done.11.refs_0_ = bf16[128,1536]{1,0:T(8,128)(2,1)S(1)} collective-permute-done((bf16[128,1536]{1,0:T(8,128)(2,1)}, bf16[128,1536]{1,0:T(8,128)(2,1)S(1)}, u32[]{:S(2)}, u32[]{:S(2)}) %collective-permute-start.11) | collective-permute-done | bytes 393248 | tf_op jit(solution)/shard_map/ppermute | solution.py:178
  127.4 2.7 %collective-permute-done.12.refs_1_ = bf16[128,1536]{1,0:T(8,128)(2,1)S(1)} collective-permute-done((bf16[128,1536]{1,0:T(8,128)(2,1)}, bf16[128,1536]{1,0:T(8,128)(2,1)S(1)}, u32[]{:S(2)}, u32[]{:S(2)}) %collective-permute-start.12) | collective-permute-done | bytes 393248 | tf_op jit(solution)/shard_map/ppermute | solution.py:178
  130.1 6.4 %collective-permute-done.13.refs_2_ = bf16[128,1536]{1,0:T(8,128)(2,1)S(1)} collective-permute-done((bf16[128,1536]{1,0:T(8,128)(2,1)S(1)}, bf16[128,1536]{1,0:T(8,128)(2,1)S(1)}, u32[]{:S(2)}, u32[]{:S(2)}) %collective-permute-start.13) | collective-permute-done | bytes 393248 | tf_op jit(solution)/shard_map/ppermute | solution.py:178
  136.5 0.8 copy-done.14
  137.3 2.2 %totals.2.k_ref.v_ref = bf16[128,1024]{1,0:T(8,128)(2,1)} custom-call(f32[128,1024]{1,0:T(8,128)} %copy-done, bf16[128,1536]{1,0:T(8,128)(2,1)} %copy-done.9, bf16[128,1536]{1,0:T(8,128)(2,1)} %copy-done.11, bf16[128,1536]{1,0:T(8,128)(2,1)} %copy-done.14), custom_call_target="tpu_custom_call" | custom-call | flops 2000000 | bytes 2097152 | tf_op jit(solution)/shard_map/totals/pallas_call | solution.py:128
  139.5 0.0 collective-permute-start.14
  139.5 0.7 copy.11.first_ref
  140.3 0.7 copy.12.first_ref
  141.0 0.0 collective-permute-done.18.pk_ref.pv_ref
  141.0 0.7 copy-done.8
  141.7 5.4 %attend.2.rest_0_ = bf16[2,128,4096]{2,1,0:T(8,128)(2,1)} custom-call(s32[128,1]{1,0:T(8,128)} %copy.11.first_ref, bf16[2,128,4096]{2,1,0:T(8,128)(2,1)} %bitcast.8, bf16[128,1024]{1,0:T(8,128)(2,1)} %copy-done.8, bf16[128,1024]{1,0:T(8,128)(2,1)} %totals.3.k_ref.v_ref, bf16[128,1024]{1,0:T(8,128)(2,1)} %copy-done.8, bf16[128,1024]{1,0:T(8,128)(2,1)} %totals.3.k_ref.v_ref), custom_call_target="tpu_custom_call" | custom-call | flops 536870912 | bytes 4194304 | tf_op jit(solution)/shard_map/attend/pallas_call | solution.py:164
  147.2 4.0 %collective-permute-done.14.pk_ref.pv_ref = bf16[128,1024]{1,0:T(8,128)(2,1)S(1)} collective-permute-done((bf16[128,1024]{1,0:T(8,128)(2,1)}, bf16[128,1024]{1,0:T(8,128)(2,1)S(1)}, u32[]{:S(2)}, u32[]{:S(2)}) %collective-permute-start.14) | collective-permute-done | bytes 262176 | tf_op jit(solution)/shard_map/ppermute | solution.py:178
  151.1 0.7 copy-done.7
  151.8 5.4 %attend.3 = bf16[2,128,4096]{2,1,0:T(8,128)(2,1)} custom-call(s32[128,1]{1,0:T(8,128)} %copy.12.first_ref, bf16[2,128,4096]{2,1,0:T(8,128)(2,1)} %bitcast.9, bf16[128,1024]{1,0:T(8,128)(2,1)} %copy-done.7, bf16[128,1024]{1,0:T(8,128)(2,1)} %totals.2.k_ref.v_ref, bf16[128,1024]{1,0:T(8,128)(2,1)} %copy-done.7, ...), custom_call_target="tpu_custom_call", output_to_operand_aliasing={{}: (6, {})} | custom-call | flops 536870912 | bytes 4194304 | tf_op jit(solution)/shard_map/attend/pallas_call | solution.py:164
  (28 shorter events, 0.1 us)
Async XLA Ops:
  1.9 17.1 %collective-permute-start.6 = (bf16[2,256,512]{2,1,0:T(8,128)(2,1)S(1)}, bf16[2,256,512]{2,1,0:T(8,128)(2,1)S(1)}, u32[]{:S(2)}, u32[]{:S(2)}) collective-permute-start(bf16[2,256,512]{2,1,0:T(8,128)(2,1)S(1)} %constant_dynamic-update-slice_fusion.refs_4_), channel_id=1, source_target_pairs={{0,7},{1,0},{2,1},{3,2},{4,3},{5,4},{6,5},{7,6},{8,15},{9,8},{10,9... | collective-permute-start | bytes 1572872 | tf_op jit(solution)/shard_map/ppermute | solution.py:178
  7.9 14.9 %collective-permute-start.3 = (bf16[2,256,512]{2,1,0:T(8,128)(2,1)S(1)}, bf16[2,256,512]{2,1,0:T(8,128)(2,1)S(1)}, u32[]{:S(2)}, u32[]{:S(2)}) collective-permute-start(bf16[2,256,512]{2,1,0:T(8,128)(2,1)S(1)} %constant_dynamic-update-slice_fusion.refs_4_), channel_id=1, source_target_pairs={{0,1},{1,2},{2,3},{3,4},{4,5},{5,6},{6,7},{7,0},{8,9},{9,10},{10,1... | collective-permute-start | bytes 1572872 | tf_op jit(solution)/shard_map/ppermute | solution.py:178
  19.1 17.0 %collective-permute-start.7 = (bf16[2,256,512]{2,1,0:T(8,128)(2,1)S(1)}, bf16[2,256,512]{2,1,0:T(8,128)(2,1)}, u32[]{:S(2)}, u32[]{:S(2)}) collective-permute-start(bf16[2,256,512]{2,1,0:T(8,128)(2,1)S(1)} %collective-permute-done.6.refs_8_), channel_id=1, source_target_pairs={{0,7},{1,0},{2,1},{3,2},{4,3},{5,4},{6,5},{7,6},{8,15},{9,8},{10,9... | collective-permute-start | bytes 1572872 | tf_op jit(solution)/shard_map/ppermute | solution.py:178
  22.8 7.4 %copy-start.3 = (bf16[2,256,512]{2,1,0:T(8,128)(2,1)}, bf16[2,256,512]{2,1,0:T(8,128)(2,1)S(1)}, u32[]{:S(2)}) copy-start(bf16[2,256,512]{2,1,0:T(8,128)(2,1)S(1)} %collective-permute-done.3.refs_5_) | copy-start | bytes 1572868
  22.8 16.3 %collective-permute-start.4 = (bf16[2,256,512]{2,1,0:T(8,128)(2,1)S(1)}, bf16[2,256,512]{2,1,0:T(8,128)(2,1)}, u32[]{:S(2)}, u32[]{:S(2)}) collective-permute-start(bf16[2,256,512]{2,1,0:T(8,128)(2,1)S(1)} %collective-permute-done.3.refs_5_), channel_id=1, source_target_pairs={{0,1},{1,2},{2,3},{3,4},{4,5},{5,6},{6,7},{7,0},{8,9},{9,10},{10,1... | collective-permute-start | bytes 1572872 | tf_op jit(solution)/shard_map/ppermute | solution.py:178
  22.8 30.0 %copy-start.16 = (s32[8]{0:T(128)S(1)}, s32[8]{0:T(128)}, u32[]{:S(2)}) copy-start(s32[8]{0:T(128)} %constant.38) | copy-start | bytes 100
  30.1 49.1 %copy-start.2 = (bf16[256,2048]{1,0:T(8,128)(2,1)S(1)}, bf16[256,2048]{1,0:T(8,128)(2,1)}, u32[]{:S(2)}) copy-start(bf16[256,2048]{1,0:T(8,128)(2,1)} %get-tuple-element.17.refs_0_) | copy-start | bytes 3145732
  30.1 31.6 %collective-permute-start = (bf16[256,2048]{1,0:T(8,128)(2,1)}, bf16[256,2048]{1,0:T(8,128)(2,1)}, u32[]{:S(2)}, u32[]{:S(2)}) collective-permute-start(bf16[256,2048]{1,0:T(8,128)(2,1)} %get-tuple-element.18), channel_id=1, source_target_pairs={{0,8},{8,16},{16,24},{24,0},{1,9},{9,17},{17,25},{25,1},{2,10},{10... | collective-permute-start | bytes 3145736 | tf_op jit(solution)/shard_map/ppermute | solution.py:178
  31.8 47.4 %collective-permute-start.1 = (bf16[256,2048]{1,0:T(8,128)(2,1)}, bf16[256,2048]{1,0:T(8,128)(2,1)}, u32[]{:S(2)}, u32[]{:S(2)}) collective-permute-start(bf16[256,2048]{1,0:T(8,128)(2,1)} %get-tuple-element.19), channel_id=1, source_target_pairs={{0,16},{8,24},{16,0},{24,8},{1,17},{9,25},{17,1},{25,9},{2,18},{10... | collective-permute-start | bytes 3145736 | tf_op jit(solution)/shard_map/ppermute | solution.py:178
  34.7 44.5 %collective-permute-start.2 = (bf16[256,2048]{1,0:T(8,128)(2,1)}, bf16[256,2048]{1,0:T(8,128)(2,1)}, u32[]{:S(2)}, u32[]{:S(2)}) collective-permute-start(bf16[256,2048]{1,0:T(8,128)(2,1)} %get-tuple-element.20), channel_id=1, source_target_pairs={{0,24},{8,0},{16,8},{24,16},{1,25},{9,1},{17,9},{25,17},{2,26},{10... | collective-permute-start | bytes 3145736 | tf_op jit(solution)/shard_map/ppermute | solution.py:178
  36.1 12.3 %collective-permute-start.8 = (bf16[2,256,512]{2,1,0:T(8,128)(2,1)}, bf16[2,256,512]{2,1,0:T(8,128)(2,1)S(1)}, u32[]{:S(2)}, u32[]{:S(2)}) collective-permute-start(bf16[2,256,512]{2,1,0:T(8,128)(2,1)} %collective-permute-done.7.refs_9_), channel_id=1, source_target_pairs={{0,7},{1,0},{2,1},{3,2},{4,3},{5,4},{6,5},{7,6},{8,15},{9,8},{10,9... | collective-permute-start | bytes 1572872 | tf_op jit(solution)/shard_map/ppermute | solution.py:178
  39.1 12.9 %collective-permute-start.5 = (bf16[2,256,512]{2,1,0:T(8,128)(2,1)}, bf16[2,256,512]{2,1,0:T(8,128)(2,1)S(1)}, u32[]{:S(2)}, u32[]{:S(2)}) collective-permute-start(bf16[2,256,512]{2,1,0:T(8,128)(2,1)} %collective-permute-done.4.refs_6_), channel_id=1, source_target_pairs={{0,1},{1,2},{2,3},{3,4},{4,5},{5,6},{6,7},{7,0},{8,9},{9,10},{10,1... | collective-permute-start | bytes 1572872 | tf_op jit(solution)/shard_map/ppermute | solution.py:178
  48.4 7.6 %collective-permute-start.10 = (bf16[1,256,512]{2,1,0:T(8,128)(2,1)S(1)}, bf16[1,256,512]{2,1,0:T(8,128)(2,1)}, u32[]{:S(2)}, u32[]{:S(2)}) collective-permute-start(bf16[1,256,512]{2,1,0:T(8,128)(2,1)S(1)} %slice.19), channel_id=1, source_target_pairs={{0,7},{1,0},{2,1},{3,2},{4,3},{5,4},{6,5},{7,6},{8,15},{9,8},{10,9... | collective-permute-start | bytes 786440 | tf_op jit(solution)/shard_map/ppermute | solution.py:178
  52.8 7.9 %collective-permute-start.9 = (bf16[1,256,512]{2,1,0:T(8,128)(2,1)}, bf16[1,256,512]{2,1,0:T(8,128)(2,1)}, u32[]{:S(2)}, u32[]{:S(2)}) collective-permute-start(bf16[1,256,512]{2,1,0:T(8,128)(2,1)} %slice.18), channel_id=1, source_target_pairs={{0,1},{1,2},{2,3},{3,4},{4,5},{5,6},{6,7},{7,0},{8,9},{9,10},{10,1... | collective-permute-start | bytes 786440 | tf_op jit(solution)/shard_map/ppermute | solution.py:178
  79.2 1.0 copy-start.4
  80.3 14.8 %copy-start.15 = (s32[2,64]{1,0:T(2,128)S(1)}, s32[2,64]{1,0:T(2,128)}, u32[]{:S(2)}) copy-start(s32[2,64]{1,0:T(2,128)} %param.12) | copy-start | bytes 1540
  88.0 0.8 copy-start
  88.8 0.8 copy-start.1
  89.6 0.8 copy-start.5
  90.4 0.7 copy-start.6
  91.1 20.3 %collective-permute-start.15 = (bf16[128,1536]{1,0:T(8,128)(2,1)}, bf16[128,1536]{1,0:T(8,128)(2,1)S(1)}, u32[]{:S(2)}, u32[]{:S(2)}) collective-permute-start(bf16[128,1536]{1,0:T(8,128)(2,1)} %get-tuple-element.26), channel_id=1, source_target_pairs={{0,24},{8,0},{16,8},{24,16},{1,25},{9,1},{17,9},{25,17},{2,26},{10... | collective-permute-start | bytes 1179656 | tf_op jit(solution)/shard_map/ppermute | solution.py:178
  93.3 19.0 %collective-permute-start.16 = (bf16[128,1536]{1,0:T(8,128)(2,1)}, bf16[128,1536]{1,0:T(8,128)(2,1)S(1)}, u32[]{:S(2)}, u32[]{:S(2)}) collective-permute-start(bf16[128,1536]{1,0:T(8,128)(2,1)} %get-tuple-element.27), channel_id=1, source_target_pairs={{0,16},{8,24},{16,0},{24,8},{1,17},{9,25},{17,1},{25,9},{2,18},{10... | collective-permute-start | bytes 1179656 | tf_op jit(solution)/shard_map/ppermute | solution.py:178
  94.4 21.0 %collective-permute-start.17 = (bf16[128,1536]{1,0:T(8,128)(2,1)}, bf16[128,1536]{1,0:T(8,128)(2,1)S(1)}, u32[]{:S(2)}, u32[]{:S(2)}) collective-permute-start(bf16[128,1536]{1,0:T(8,128)(2,1)} %get-tuple-element.28), channel_id=1, source_target_pairs={{0,8},{8,16},{16,24},{24,0},{1,9},{9,17},{17,25},{25,1},{2,10},{10... | collective-permute-start | bytes 1179656 | tf_op jit(solution)/shard_map/ppermute | solution.py:178
  95.2 32.2 %collective-permute-start.11 = (bf16[128,1536]{1,0:T(8,128)(2,1)}, bf16[128,1536]{1,0:T(8,128)(2,1)S(1)}, u32[]{:S(2)}, u32[]{:S(2)}) collective-permute-start(bf16[128,1536]{1,0:T(8,128)(2,1)} %copy-done.6), channel_id=1, source_target_pairs={{0,24},{8,0},{16,8},{24,16},{1,25},{9,1},{17,9},{25,17},{2,26},{10... | collective-permute-start | bytes 1179656 | tf_op jit(solution)/shard_map/ppermute | solution.py:178
  97.9 32.2 %collective-permute-start.12 = (bf16[128,1536]{1,0:T(8,128)(2,1)}, bf16[128,1536]{1,0:T(8,128)(2,1)S(1)}, u32[]{:S(2)}, u32[]{:S(2)}) collective-permute-start(bf16[128,1536]{1,0:T(8,128)(2,1)} %copy-done.5), channel_id=1, source_target_pairs={{0,16},{8,24},{16,0},{24,8},{1,17},{9,25},{17,1},{25,9},{2,18},{10... | collective-permute-start | bytes 1179656 | tf_op jit(solution)/shard_map/ppermute | solution.py:178
  111.4 4.1 %copy-start.10 = (bf16[128,1536]{1,0:T(8,128)(2,1)}, bf16[128,1536]{1,0:T(8,128)(2,1)S(1)}, u32[]{:S(2)}) copy-start(bf16[128,1536]{1,0:T(8,128)(2,1)S(1)} %collective-permute-done.15.refs_0_) | copy-start | bytes 1179652
  111.4 25.1 %collective-permute-start.13 = (bf16[128,1536]{1,0:T(8,128)(2,1)S(1)}, bf16[128,1536]{1,0:T(8,128)(2,1)S(1)}, u32[]{:S(2)}, u32[]{:S(2)}) collective-permute-start(bf16[128,1536]{1,0:T(8,128)(2,1)S(1)} %get-tuple-element.24), channel_id=1, source_target_pairs={{0,8},{8,16},{16,24},{24,0},{1,9},{9,17},{17,25},{25,1},{2,10},{10... | collective-permute-start | bytes 1179656 | tf_op jit(solution)/shard_map/ppermute | solution.py:178
  112.3 3.2 %copy-start.12 = (bf16[128,1536]{1,0:T(8,128)(2,1)}, bf16[128,1536]{1,0:T(8,128)(2,1)S(1)}, u32[]{:S(2)}) copy-start(bf16[128,1536]{1,0:T(8,128)(2,1)S(1)} %collective-permute-done.16.refs_1_) | copy-start | bytes 1179652
  115.5 0.8 copy-start.13
  118.5 22.5 %collective-permute-start.18 = (bf16[128,1024]{1,0:T(8,128)(2,1)}, bf16[128,1024]{1,0:T(8,128)(2,1)S(1)}, u32[]{:S(2)}, u32[]{:S(2)}) collective-permute-start(bf16[128,1024]{1,0:T(8,128)(2,1)} %totals.3.k_ref.v_ref), channel_id=1, source_target_pairs={{0,1},{1,2},{2,3},{3,4},{4,5},{5,6},{6,7},{7,8},{8,9},{9,10},{10,1... | collective-permute-start | bytes 786440 | tf_op jit(solution)/shard_map/ppermute | solution.py:178
  127.4 9.1 %copy-start.9 = (bf16[128,1536]{1,0:T(8,128)(2,1)}, bf16[128,1536]{1,0:T(8,128)(2,1)S(1)}, u32[]{:S(2)}) copy-start(bf16[128,1536]{1,0:T(8,128)(2,1)S(1)} %collective-permute-done.11.refs_0_) | copy-start | bytes 1179652
  130.1 6.4 %copy-start.11 = (bf16[128,1536]{1,0:T(8,128)(2,1)}, bf16[128,1536]{1,0:T(8,128)(2,1)S(1)}, u32[]{:S(2)}) copy-start(bf16[128,1536]{1,0:T(8,128)(2,1)S(1)} %collective-permute-done.12.refs_1_) | copy-start | bytes 1179652
  136.5 0.8 copy-start.14
  139.5 11.6 %collective-permute-start.14 = (bf16[128,1024]{1,0:T(8,128)(2,1)}, bf16[128,1024]{1,0:T(8,128)(2,1)S(1)}, u32[]{:S(2)}, u32[]{:S(2)}) collective-permute-start(bf16[128,1024]{1,0:T(8,128)(2,1)} %totals.2.k_ref.v_ref), channel_id=1, source_target_pairs={{0,1},{1,2},{2,3},{3,4},{4,5},{5,6},{6,7},{7,8},{8,9},{9,10},{10,1... | collective-permute-start | bytes 786440 | tf_op jit(solution)/shard_map/ppermute | solution.py:178
  141.0 0.7 copy-start.8
  151.1 0.7 copy-start.7

commit v2 on v1

v2 whole, which is shorter than its diff:
```python
import functools

import jax
import jax.numpy as jnp
from jax import lax
from jax.experimental import pallas as pl
from jax.experimental.pallas import tpu as pltpu
from jax.sharding import Mesh, PartitionSpec as P


HEAD = 128
Y, Z = 4, 8
VMEM = 67_043_328


def cost(flops, nbytes):
    return pl.CostEstimate(flops=flops, bytes_accessed=nbytes, transcendentals=0)


def vmem():
    return pl.BlockSpec(memory_space=pltpu.VMEM)


def hbm():
    return pl.BlockSpec(memory_space=pltpu.HBM)


def any_space():
    return pl.BlockSpec(memory_space=pl.ANY)


def pair_kernel(k_ref, v_ref, out_ref, sem):
    loads = [pltpu.make_async_copy(r.at[0], out_ref.at[i], sem.at[i]) for i, r in enumerate((k_ref, v_ref))]
    for c in loads:
        c.start()
    for c in loads:
        c.wait()


def pair(key_weight, value_weight):
    return pl.pallas_call(
        pair_kernel,
        in_specs=[hbm()] * 2,
        out_specs=vmem(),
        out_shape=jax.ShapeDtypeStruct((2,) + key_weight.shape[1:], key_weight.dtype),
        scratch_shapes=[pltpu.SemaphoreType.DMA((2,))],
        cost_estimate=cost(1_000_000, 1 << 20),
        compiler_params=pltpu.CompilerParams(vmem_limit_bytes=VMEM - (720 << 10)),
        name="pair",
    )(key_weight, value_weight)


CAME = [0] + [s + 1 for s in range(Z // 2 - 1)] + [-s - 1 for s in range(Z // 2 - 1)] + [Z // 2]
CHUNKS = 4


def norm_kernel(m, x_ref, g_ref, *refs):
    out_refs, x_buf, sem = refs[:Y], refs[Y], refs[Y + 1]
    y, z = lax.axis_index("y"), lax.axis_index("z")
    count = x_ref.shape[1] // CHUNKS
    loads = [pltpu.make_async_copy(x_ref.at[m, pl.ds(c * count, count)], x_buf.at[c], sem.at[c]) for c in range(CHUNKS)]
    for load in loads:
        load.start()
    wide = x_ref.shape[2] // (Y * Z)
    for c in range(CHUNKS):
        loads[c].wait()
        x = x_buf[c].astype(jnp.float32)
        inv = lax.rsqrt(jnp.mean(x * x, axis=-1, keepdims=True) + 1e-05)
        rows = slice(c * count, (c + 1) * count)
        for j in range(Y):
            for i in range(Z):
                at = ((y + j) & (Y - 1)) * Z + ((z - CAME[i]) & (Z - 1))
                at = pl.multiple_of(at * wide, wide)
                cols = x_buf[c, :, pl.ds(at, wide)].astype(jnp.float32)
                gain = g_ref[:, pl.ds(at, wide)].astype(jnp.float32)
                out_refs[j][rows, i * wide : (i + 1) * wide] = (cols * inv * gain).astype(jnp.bfloat16)


def norm_quarters(m, tokens, gain):
    _, count, width = tokens.shape
    return pl.pallas_call(
        functools.partial(norm_kernel, m),
        in_specs=[hbm(), vmem()],
        out_specs=[vmem()] * Y,
        out_shape=[jax.ShapeDtypeStruct((count, width // Y), jnp.bfloat16)] * Y,
        scratch_shapes=[
            pltpu.VMEM((CHUNKS, count // CHUNKS, width), jnp.bfloat16),
            pltpu.SemaphoreType.DMA((CHUNKS,)),
        ],
        cost_estimate=cost(10_000_000, 4 << 20),
        compiler_params=pltpu.CompilerParams(vmem_limit_bytes=VMEM - ((6656, 10240)[m] << 10)),
        name="norm",
    )(tokens, gain)


def product_kernel(*refs):
    a_refs, w_refs, far_refs = refs[:Y], refs[Y : Y + Z - 1], refs[Y + Z - 1 : Y + Z + 1]
    own_ref, send_refs = refs[Y + Z + 1], refs[Y + Z + 2 :]
    count, wide = a_refs[0].shape[0], w_refs[0].shape[2]
    a = jnp.concatenate([r[...] for r in a_refs], axis=0)
    wk = jnp.concatenate([r[0] for r in w_refs] + [far_refs[0][0]], axis=0)
    wv = jnp.concatenate([r[1] for r in w_refs] + [far_refs[1][0]], axis=0)
    k = jnp.dot(a, wk, preferred_element_type=jnp.float32)
    v = jnp.dot(a, wv, preferred_element_type=jnp.float32)
    own_ref[:, :wide] = k[:count]
    own_ref[:, wide:] = v[:count]
    for j in range(1, Y):
        kj, vj, out = k[j * count : (j + 1) * count], v[j * count : (j + 1) * count], send_refs[j - 1]
        high = kj.astype(jnp.bfloat16)
        out[:, :wide] = high
        out[:, wide : 2 * wide] = (kj - high.astype(jnp.float32)).astype(jnp.bfloat16)
        out[:, 2 * wide :] = vj.astype(jnp.bfloat16)


def products(acts, weights):
    rows, deep = acts[0].shape
    wide = weights[0].shape[2]
    return pl.pallas_call(
        product_kernel,
        in_specs=[vmem()] * (Y + Z + 1),
        out_specs=[vmem()] * Y,
        out_shape=[jax.ShapeDtypeStruct((rows, 2 * wide), jnp.float32)]
        + [jax.ShapeDtypeStruct((rows, 3 * wide), jnp.bfloat16)] * (Y - 1),
        cost_estimate=cost(4 * Y * rows * deep * wide, 8 << 20),
        compiler_params=pltpu.CompilerParams(vmem_limit_bytes=20 << 20),
        name="products",
    )(*acts, *weights)


def total_kernel(own_ref, *refs):
    parts, out_ref = refs[:3], refs[3]
    wide = own_ref.shape[1] // 2
    k, v = own_ref[:, :wide], own_ref[:, wide:]
    for p in parts:
        k = k + (p[:, :wide].astype(jnp.float32) + p[:, wide : 2 * wide].astype(jnp.float32))
        v = v + p[:, 2 * wide :].astype(jnp.float32)
    out_ref[:, :wide] = k.astype(jnp.bfloat16)
    out_ref[:, wide:] = v.astype(jnp.bfloat16)


def totals(own, parts):
    return pl.pallas_call(
        total_kernel,
        in_specs=[vmem()] * 4,
        out_specs=vmem(),
        out_shape=jax.ShapeDtypeStruct(own.shape, jnp.bfloat16),
        cost_estimate=cost(2_000_000, 2 << 20),
        compiler_params=pltpu.CompilerParams(vmem_limit_bytes=6 << 20),
        name="totals",
    )(own, *parts)


def attend_kernel(slot, len_ref, q_ref, pk_ref, k_ref, pv_ref, v_ref, *rest):
    out_ref = rest[-1]
    count, docs = q_ref.shape[1], len_ref.shape[1]
    before = lax.broadcasted_iota(jnp.int32, (docs, docs), 0) <= lax.broadcasted_iota(jnp.int32, (docs, docs), 1)
    lengths = len_ref[slot : slot + 1].astype(jnp.float32).astype(jnp.bfloat16)
    lengths = jnp.broadcast_to(lengths, (8, docs))
    ends = jnp.dot(lengths, before.astype(jnp.bfloat16), preferred_element_type=jnp.float32)[:1]
    ends = ends.astype(jnp.int32)
    base = (lax.axis_index("y") * Z + lax.axis_index("z")) * count
    position = base + lax.broadcasted_iota(jnp.int32, (count, docs), 0)
    first = jnp.max(jnp.where(ends <= position, ends, 0).astype(jnp.float32), axis=1, keepdims=True)
    first = first.astype(jnp.int32) - (base - count)
    column = lax.broadcasted_iota(jnp.int32, (count, 2 * count), 1)
    row = lax.broadcasted_iota(jnp.int32, (count, 2 * count), 0)
    allowed = (column >= first) & (column <= row + count)
    keys = jnp.concatenate([pk_ref[...], k_ref[...]], axis=0)
    values = jnp.concatenate([pv_ref[...], v_ref[...]], axis=0)
    values = jnp.concatenate([values, jnp.ones_like(values)], axis=1)
    for g in range(q_ref.shape[2] // HEAD):
        q = q_ref[0, :, g * HEAD : (g + 1) * HEAD]
        s = lax.dot_general(q, keys, (((1,), (1,)), ((), ())), preferred_element_type=jnp.float32)
        s = jnp.where(allowed, s * HEAD ** (-0.5), -1e30)
        e = jnp.exp(s - jnp.max(s, axis=-1, keepdims=True))
        o = jnp.dot(e.astype(jnp.bfloat16), values, preferred_element_type=jnp.float32)
        out_ref[0, :, g * HEAD : (g + 1) * HEAD] = (o[:, :HEAD] / o[:, HEAD:]).astype(jnp.bfloat16)


def attend(slot, lengths, queries, prior, own, so_far):
    count, width = queries.shape[1], queries.shape[2]
    heads = own.shape[1] // (2 * HEAD)
    group = width // heads
    q_spec = pl.BlockSpec((1, count, group), lambda h: (slot, 0, h))
    k_spec = pl.BlockSpec((count, HEAD), lambda h: (0, h))
    v_spec = pl.BlockSpec((count, HEAD), lambda h: (0, h + heads))
    extra = [] if so_far is None else [so_far]
    return pl.pallas_call(
        functools.partial(attend_kernel, slot),
        grid=(heads,),
        in_specs=[
            pl.BlockSpec(lengths.shape, lambda h: (0, 0)),
            q_spec,
            k_spec,
            k_spec,
            v_spec,
            v_spec,
        ]
        + [any_space()] * len(extra),
        out_specs=q_spec,
        out_shape=jax.ShapeDtypeStruct(queries.shape, jnp.bfloat16),
        input_output_aliases={6: 0} if extra else {},
        cost_estimate=cost(8 * count * count * width, 4 << 20),
        compiler_params=pltpu.CompilerParams(vmem_limit_bytes=10 << 20),
        name="attend",
    )(lengths, queries, prior, own, prior, own, *extra)


def hop(block, axis, count, distance, closed=True):
    return lax.ppermute(block, axis, [(i, (i + distance) % count) for i in range(count) if closed or i + distance < count])


def body(tokens, queries, gains, key_weight, value_weight, lengths):
    slots, _, _ = tokens.shape[1:]
    steps = Z // 2 - 1

    own_w = pair(key_weight, value_weight)
    up = down = own_w
    ups, downs = [], []
    for _ in range(steps):
        up = hop(up, "z", Z, 1)
        down = hop(down, "z", Z, -1)
        ups.append(up)
        downs.append(down)
    far_k = hop(up[:1], "z", Z, 1)
    far_v = hop(down[1:], "z", Z, -1)
    weights = [own_w] + ups + downs + [far_k, far_v]

    acts = []
    for m in range(slots):
        quarters = norm_quarters(m, tokens[0], gains)
        acts.append([quarters[0]] + [hop(quarters[j], "y", Y, j) for j in range(1, Y)])

    owns, parts = [], []
    for m in range(slots):
        own, *send = products(acts[m], weights)
        owns.append(own)
        parts.append([hop(send[j - 1], "y", Y, -j) for j in range(1, Y)])
    out = None
    for m in range(slots):
        own = totals(owns[m], parts[m])
        prior = hop(own, ("y", "z"), Y * Z, 1, closed=False)
        out = attend(m, lengths, queries[0], prior, own, out)
    return out[None]


def solution(mesh):
    split = Mesh(mesh.devices.reshape(-1, Y, Z), ("section", "y", "z"))
    spread = ("y", "z")

    return jax.shard_map(
        body,
        mesh=split,
        in_specs=(
            P("section", None, spread, None),
            P("section", None, spread, None),
            P("section", None),
            P("section", spread, None),
            P("section", spread, None),
            P(),
        ),
        out_specs=P("section", None, spread, None),
        check_vma=False,
    )
```

time: 158 us -> 142 us (0.90)
  the two profiles are of different devices: /device:TPU:4 before, /device:TPU:8 now
where the time goes in v2:
time: 142 us; the launch traced here: 141 us
  waiting for transfers between devices  80.9 us (57%)
  starting transfers between devices  36.9 us (26%)
  Pallas kernels  23.2 us (16%)
    ppermute x22, waiting for transfers between devices, hop(): lax.ppermute(block, axis, [(i, (i + distance) % count) for i in range(cou...  80.9 us
    ppermute x22, starting transfers between devices, hop(): lax.ppermute(block, axis, [(i, (i + distance) % count) for i in range(cou...  36.9 us
    pallas_call x2, Pallas kernels, norm_quarters(): pl.pallas_call(functools.partial(norm_kernel, m), in_specs=[hbm(), vmem()...  8.5 us
    pallas_call x2, Pallas kernels, attend(): pl.pallas_call(functools.partial(attend_kernel, slot), grid=(heads,), in_...  7.8 us
    pallas_call x2, Pallas kernels, products(): pl.pallas_call(product_kernel, in_specs=[vmem()] * (Y + Z + 1), out_specs...  4.67 us
  transfers between devices with their start and end apart: 22, of which 13 were waited for; matrix products, arithmetic and copies ran while one was open for 0% of the time, Pallas kernels for 12%

profile of v2, /device:TPU:8, one launch (start us, length us, event | category | flops | bytes accessed | tf_op | source)
XLA Modules:
  0.0 141.3 jit_solution(2386947997364915456)
XLA Ops:
  0.0 1.9 %pair.1.refs_4_ = bf16[2,256,512]{2,1,0:T(8,128)(2,1)} custom-call(bf16[1,256,512]{2,1,0:T(8,128)(2,1)} %k_ref.1, bf16[1,256,512]{2,1,0:T(8,128)(2,1)} %v_ref.1), custom_call_target="tpu_custom_call" | custom-call | flops 1000000 | bytes 1048576 | tf_op jit(solution)/shard_map/pair/pallas_call | solution.py:41
  1.9 2.0 %collective-permute-start.3 = (bf16[2,256,512]{2,1,0:T(8,128)(2,1)}, bf16[2,256,512]{2,1,0:T(8,128)(2,1)S(1)}, u32[]{:S(2)}, u32[]{:S(2)}) collective-permute-start(bf16[2,256,512]{2,1,0:T(8,128)(2,1)} %pair.1.refs_4_), channel_id=1, source_target_pairs={{0,1},{1,2},{2,3},{3,4},{4,5},{5,6},{6,7},{7,0},{8,9},{9,10},{10,1... | collective-permute-start | bytes 1572872 | tf_op jit(solution)/shard_map/ppermute | solution.py:210
  3.9 4.0 %collective-permute-start.6 = (bf16[2,256,512]{2,1,0:T(8,128)(2,1)}, bf16[2,256,512]{2,1,0:T(8,128)(2,1)S(1)}, u32[]{:S(2)}, u32[]{:S(2)}) collective-permute-start(bf16[2,256,512]{2,1,0:T(8,128)(2,1)} %pair.1.refs_4_), channel_id=1, source_target_pairs={{0,7},{1,0},{2,1},{3,2},{4,3},{5,4},{6,5},{7,6},{8,15},{9,8},{10,9... | collective-permute-start | bytes 1572872 | tf_op jit(solution)/shard_map/ppermute | solution.py:210
  7.9 12.0 %collective-permute-done.3.refs_5_ = bf16[2,256,512]{2,1,0:T(8,128)(2,1)S(1)} collective-permute-done((bf16[2,256,512]{2,1,0:T(8,128)(2,1)}, bf16[2,256,512]{2,1,0:T(8,128)(2,1)S(1)}, u32[]{:S(2)}, u32[]{:S(2)}) %collective-permute-start.3) | collective-permute-done | bytes 524320 | tf_op jit(solution)/shard_map/ppermute | solution.py:210
  19.9 0.0 collective-permute-start.4
  19.9 0.0 collective-permute-done.6.refs_8_
  19.9 3.2 %collective-permute-start.7 = (bf16[2,256,512]{2,1,0:T(8,128)(2,1)S(1)}, bf16[2,256,512]{2,1,0:T(8,128)(2,1)S(1)}, u32[]{:S(2)}, u32[]{:S(2)}) collective-permute-start(bf16[2,256,512]{2,1,0:T(8,128)(2,1)S(1)} %collective-permute-done.6.refs_8_), channel_id=1, source_target_pairs={{0,7},{1,0},{2,1},{3,2},{4,3},{5,4},{6,5},{7,6},{8,15},{9,8},{10,9... | collective-permute-start | bytes 1572872 | tf_op jit(solution)/shard_map/ppermute | solution.py:210
  23.2 11.1 %collective-permute-done.4.refs_6_ = bf16[2,256,512]{2,1,0:T(8,128)(2,1)S(1)} collective-permute-done((bf16[2,256,512]{2,1,0:T(8,128)(2,1)S(1)}, bf16[2,256,512]{2,1,0:T(8,128)(2,1)S(1)}, u32[]{:S(2)}, u32[]{:S(2)}) %collective-permute-start.4) | collective-permute-done | bytes 524320 | tf_op jit(solution)/shard_map/ppermute | solution.py:210
  34.2 0.0 collective-permute-start.5
  34.2 0.0 collective-permute-done.7.refs_9_
  34.2 3.2 %collective-permute-start.8 = (bf16[2,256,512]{2,1,0:T(8,128)(2,1)S(1)}, bf16[2,256,512]{2,1,0:T(8,128)(2,1)S(1)}, u32[]{:S(2)}, u32[]{:S(2)}) collective-permute-start(bf16[2,256,512]{2,1,0:T(8,128)(2,1)S(1)} %collective-permute-done.7.refs_9_), channel_id=1, source_target_pairs={{0,7},{1,0},{2,1},{3,2},{4,3},{5,4},{6,5},{7,6},{8,15},{9,8},{10,9... | collective-permute-start | bytes 1572872 | tf_op jit(solution)/shard_map/ppermute | solution.py:210
  37.5 4.2 %norm.3 = (bf16[128,2048]{1,0:T(8,128)(2,1)}, bf16[128,2048]{1,0:T(8,128)(2,1)}, bf16[128,2048]{1,0:T(8,128)(2,1)}, bf16[128,2048]{1,0:T(8,128)(2,1)}) custom-call(bf16[2,128,8192]{2,1,0:T(8,128)(2,1)} %bitcast.5, bf16[1,8192]{1,0:T(2,128)(2,1)} %g_ref.3), custom_call_target="tpu_custom_call" | custom-call | flops 10000000 | bytes 4194304 | tf_op jit(solution)/shard_map/norm/pallas_call | solution.py:81
  41.7 1.7 %collective-permute-start.15 = (bf16[128,2048]{1,0:T(8,128)(2,1)}, bf16[128,2048]{1,0:T(8,128)(2,1)S(1)}, u32[]{:S(2)}, u32[]{:S(2)}) collective-permute-start(bf16[128,2048]{1,0:T(8,128)(2,1)} %get-tuple-element.30), channel_id=1, source_target_pairs={{0,8},{8,16},{16,24},{24,0},{1,9},{9,17},{17,25},{25,1},{2,10},{10... | collective-permute-start | bytes 1572872 | tf_op jit(solution)/shard_map/ppermute | solution.py:210
  43.4 0.9 collective-permute-start.16
  44.3 2.4 %collective-permute-start.17 = (bf16[128,2048]{1,0:T(8,128)(2,1)}, bf16[128,2048]{1,0:T(8,128)(2,1)S(1)}, u32[]{:S(2)}, u32[]{:S(2)}) collective-permute-start(bf16[128,2048]{1,0:T(8,128)(2,1)} %get-tuple-element.32), channel_id=1, source_target_pairs={{0,24},{8,0},{16,8},{24,16},{1,25},{9,1},{17,9},{25,17},{2,26},{10... | collective-permute-start | bytes 1572872 | tf_op jit(solution)/shard_map/ppermute | solution.py:210
  46.7 0.9 collective-permute-done.5.refs_7_
  47.7 0.1 collective-permute-start.9
  47.8 0.0 collective-permute-done.8.refs_10_
  47.8 0.0 copy-start.1
  47.8 0.0 copy-start.4
  47.9 3.3 %collective-permute-start.10 = (bf16[1,256,512]{2,1,0:T(8,128)(2,1)S(1)}, bf16[1,256,512]{2,1,0:T(8,128)(2,1)S(1)}, u32[]{:S(2)}, u32[]{:S(2)}) collective-permute-start(bf16[1,256,512]{2,1,0:T(8,128)(2,1)S(1)} %slice.9), channel_id=1, source_target_pairs={{0,7},{1,0},{2,1},{3,2},{4,3},{5,4},{6,5},{7,6},{8,15},{9,8},{10,9... | collective-permute-start | bytes 786440 | tf_op jit(solution)/shard_map/ppermute | solution.py:210
  51.1 4.3 %norm.2 = (bf16[128,2048]{1,0:T(8,128)(2,1)}, bf16[128,2048]{1,0:T(8,128)(2,1)}, bf16[128,2048]{1,0:T(8,128)(2,1)}, bf16[128,2048]{1,0:T(8,128)(2,1)}) custom-call(bf16[2,128,8192]{2,1,0:T(8,128)(2,1)} %bitcast.6, bf16[1,8192]{1,0:T(2,128)(2,1)} %g_ref.3), custom_call_target="tpu_custom_call" | custom-call | flops 10000000 | bytes 4194304 | tf_op jit(solution)/shard_map/norm/pallas_call | solution.py:81
  55.4 6.8 %collective-permute-done.15.refs_1_ = bf16[128,2048]{1,0:T(8,128)(2,1)S(1)} collective-permute-done((bf16[128,2048]{1,0:T(8,128)(2,1)}, bf16[128,2048]{1,0:T(8,128)(2,1)S(1)}, u32[]{:S(2)}, u32[]{:S(2)}) %collective-permute-start.15) | collective-permute-done | bytes 524320 | tf_op jit(solution)/shard_map/ppermute | solution.py:210
  62.2 2.9 %collective-permute-start = (bf16[128,2048]{1,0:T(8,128)(2,1)}, bf16[128,2048]{1,0:T(8,128)(2,1)S(1)}, u32[]{:S(2)}, u32[]{:S(2)}) collective-permute-start(bf16[128,2048]{1,0:T(8,128)(2,1)} %get-tuple-element.22), channel_id=1, source_target_pairs={{0,8},{8,16},{16,24},{24,0},{1,9},{9,17},{17,25},{25,1},{2,10},{10... | collective-permute-start | bytes 1572872 | tf_op jit(solution)/shard_map/ppermute | solution.py:210
  65.1 0.0 collective-permute-done.16.refs_2_
  65.1 0.0 collective-permute-start.1
  65.1 4.6 %collective-permute-done.17.refs_3_ = bf16[128,2048]{1,0:T(8,128)(2,1)S(1)} collective-permute-done((bf16[128,2048]{1,0:T(8,128)(2,1)}, bf16[128,2048]{1,0:T(8,128)(2,1)S(1)}, u32[]{:S(2)}, u32[]{:S(2)}) %collective-permute-start.17) | collective-permute-done | bytes 524320 | tf_op jit(solution)/shard_map/ppermute | solution.py:210
  69.7 2.0 %collective-permute-start.2 = (bf16[128,2048]{1,0:T(8,128)(2,1)}, bf16[128,2048]{1,0:T(8,128)(2,1)S(1)}, u32[]{:S(2)}, u32[]{:S(2)}) collective-permute-start(bf16[128,2048]{1,0:T(8,128)(2,1)} %get-tuple-element.24), channel_id=1, source_target_pairs={{0,24},{8,0},{16,8},{24,16},{1,25},{9,1},{17,9},{25,17},{2,26},{10... | collective-permute-start | bytes 1572872 | tf_op jit(solution)/shard_map/ppermute | solution.py:210
  71.6 0.0 collective-permute-done.9.refs_11_
  71.6 0.0 collective-permute-done.10.refs_12_
  71.6 0.0 copy-done.1
  71.6 0.0 copy-done.4
  71.7 0.0 copy-start.3
  71.7 2.3 %products.3 = (f32[128,1024]{1,0:T(8,128)S(1)}, bf16[128,1536]{1,0:T(8,128)(2,1)S(1)}, bf16[128,1536]{1,0:T(8,128)(2,1)S(1)}, bf16[128,1536]{1,0:T(8,128)(2,1)S(1)}) custom-call(bf16[128,2048]{1,0:T(8,128)(2,1)S(1)} %copy-done.4, bf16[128,2048]{1,0:T(8,128)(2,1)S(1)} %collective-permute-done.15.refs_1_, ...), custom_call_target="tpu_custom_call" | custom-call | flops 2147483648 | bytes 8388608 | tf_op jit(solution)/shard_map/products/pallas_call | solution.py:118
  74.0 1.6 %collective-permute-start.18 = (bf16[128,1536]{1,0:T(8,128)(2,1)S(1)}, bf16[128,1536]{1,0:T(8,128)(2,1)S(1)}, u32[]{:S(2)}, u32[]{:S(2)}) collective-permute-start(bf16[128,1536]{1,0:T(8,128)(2,1)S(1)} %get-tuple-element.34), channel_id=1, source_target_pairs={{0,24},{8,0},{16,8},{24,16},{1,25},{9,1},{17,9},{25,17},{2,26},{10... | collective-permute-start | bytes 1179656 | tf_op jit(solution)/shard_map/ppermute | solution.py:210
  75.7 0.8 collective-permute-start.19
  76.5 16.7 %collective-permute-done.refs_1_ = bf16[128,2048]{1,0:T(8,128)(2,1)S(1)} collective-permute-done((bf16[128,2048]{1,0:T(8,128)(2,1)}, bf16[128,2048]{1,0:T(8,128)(2,1)S(1)}, u32[]{:S(2)}, u32[]{:S(2)}) %collective-permute-start) | collective-permute-done | bytes 524320 | tf_op jit(solution)/shard_map/ppermute | solution.py:210
  93.2 2.9 %collective-permute-start.20 = (bf16[128,1536]{1,0:T(8,128)(2,1)S(1)}, bf16[128,1536]{1,0:T(8,128)(2,1)S(1)}, u32[]{:S(2)}, u32[]{:S(2)}) collective-permute-start(bf16[128,1536]{1,0:T(8,128)(2,1)S(1)} %get-tuple-element.36), channel_id=1, source_target_pairs={{0,8},{8,16},{16,24},{24,0},{1,9},{9,17},{17,25},{25,1},{2,10},{10... | collective-permute-start | bytes 1179656 | tf_op jit(solution)/shard_map/ppermute | solution.py:210
  96.1 0.0 collective-permute-done.1.refs_2_
  96.1 0.0 collective-permute-done.2.refs_3_
  96.1 0.0 copy-done.3
  96.1 2.3 %products.2 = (f32[128,1024]{1,0:T(8,128)S(1)}, bf16[128,1536]{1,0:T(8,128)(2,1)S(1)}, bf16[128,1536]{1,0:T(8,128)(2,1)S(1)}, bf16[128,1536]{1,0:T(8,128)(2,1)S(1)}) custom-call(bf16[128,2048]{1,0:T(8,128)(2,1)S(1)} %copy-done.3, bf16[128,2048]{1,0:T(8,128)(2,1)S(1)} %collective-permute-done.refs_1_, bf16[128,2048]{1,0:T(8,128)(2,1)S(1)} %collective-permute-done.1.refs_2_, ...), custom_call_target="tpu_custom_call" | custom-call | flops 2147483648 | bytes 8388608 | tf_op jit(solution)/shard_map/products/pallas_call | solution.py:118
  98.4 0.0 copy-start
  98.4 0.0 copy-start.2
  98.4 0.1 collective-permute-start.11
  98.5 1.5 %collective-permute-start.12 = (bf16[128,1536]{1,0:T(8,128)(2,1)S(1)}, bf16[128,1536]{1,0:T(8,128)(2,1)S(1)}, u32[]{:S(2)}, u32[]{:S(2)}) collective-permute-start(bf16[128,1536]{1,0:T(8,128)(2,1)S(1)} %get-tuple-element.27), channel_id=1, source_target_pairs={{0,16},{8,24},{16,0},{24,8},{1,17},{9,25},{17,1},{25,9},{2,18},{10... | collective-permute-start | bytes 1179656 | tf_op jit(solution)/shard_map/ppermute | solution.py:210
  100.0 2.2 %collective-permute-done.18.refs_0_ = bf16[128,1536]{1,0:T(8,128)(2,1)S(1)} collective-permute-done((bf16[128,1536]{1,0:T(8,128)(2,1)S(1)}, bf16[128,1536]{1,0:T(8,128)(2,1)S(1)}, u32[]{:S(2)}, u32[]{:S(2)}) %collective-permute-start.18) | collective-permute-done | bytes 393248 | tf_op jit(solution)/shard_map/ppermute | solution.py:210
  102.1 0.5 collective-permute-start.13
  102.6 7.9 %collective-permute-done.19.refs_1_ = bf16[128,1536]{1,0:T(8,128)(2,1)S(1)} collective-permute-done((bf16[128,1536]{1,0:T(8,128)(2,1)S(1)}, bf16[128,1536]{1,0:T(8,128)(2,1)S(1)}, u32[]{:S(2)}, u32[]{:S(2)}) %collective-permute-start.19) | collective-permute-done | bytes 393248 | tf_op jit(solution)/shard_map/ppermute | solution.py:210
  110.5 4.8 %collective-permute-done.20.refs_2_ = bf16[128,1536]{1,0:T(8,128)(2,1)S(1)} collective-permute-done((bf16[128,1536]{1,0:T(8,128)(2,1)S(1)}, bf16[128,1536]{1,0:T(8,128)(2,1)S(1)}, u32[]{:S(2)}, u32[]{:S(2)}) %collective-permute-start.20) | collective-permute-done | bytes 393248 | tf_op jit(solution)/shard_map/ppermute | solution.py:210
  115.4 0.2 totals.3.k_ref.v_ref
  115.5 1.9 %collective-permute-start.21 = (bf16[128,1024]{1,0:T(8,128)(2,1)S(1)}, bf16[128,1024]{1,0:T(8,128)(2,1)S(1)}, u32[]{:S(2)}, u32[]{:S(2)}) collective-permute-start(bf16[128,1024]{1,0:T(8,128)(2,1)S(1)} %totals.3.k_ref.v_ref), channel_id=1, source_target_pairs={{0,1},{1,2},{2,3},{3,4},{4,5},{5,6},{6,7},{7,8},{8,9},{9,10},{10,1... | collective-permute-start | bytes 786440 | tf_op jit(solution)/shard_map/ppermute | solution.py:210
  117.4 1.2 collective-permute-done.11.refs_0_
  118.7 5.4 %collective-permute-done.12.refs_1_ = bf16[128,1536]{1,0:T(8,128)(2,1)S(1)} collective-permute-done((bf16[128,1536]{1,0:T(8,128)(2,1)S(1)}, bf16[128,1536]{1,0:T(8,128)(2,1)S(1)}, u32[]{:S(2)}, u32[]{:S(2)}) %collective-permute-start.12) | collective-permute-done | bytes 393248 | tf_op jit(solution)/shard_map/ppermute | solution.py:210
  124.0 2.8 %collective-permute-done.13.refs_2_ = bf16[128,1536]{1,0:T(8,128)(2,1)S(1)} collective-permute-done((bf16[128,1536]{1,0:T(8,128)(2,1)S(1)}, bf16[128,1536]{1,0:T(8,128)(2,1)S(1)}, u32[]{:S(2)}, u32[]{:S(2)}) %collective-permute-start.13) | collective-permute-done | bytes 393248 | tf_op jit(solution)/shard_map/ppermute | solution.py:210
  126.9 0.2 totals.2.k_ref.v_ref
  127.0 1.9 %collective-permute-start.14 = (bf16[128,1024]{1,0:T(8,128)(2,1)S(1)}, bf16[128,1024]{1,0:T(8,128)(2,1)S(1)}, u32[]{:S(2)}, u32[]{:S(2)}) collective-permute-start(bf16[128,1024]{1,0:T(8,128)(2,1)S(1)} %totals.2.k_ref.v_ref), channel_id=1, source_target_pairs={{0,1},{1,2},{2,3},{3,4},{4,5},{5,6},{6,7},{7,8},{8,9},{9,10},{10,1... | collective-permute-start | bytes 786440 | tf_op jit(solution)/shard_map/ppermute | solution.py:210
  129.0 0.0 collective-permute-done.21.pk_ref.pv_ref
  129.0 0.0 copy-done
  129.0 0.0 copy-done.2
  129.0 3.9 %attend.2.rest_0_ = bf16[2,128,4096]{2,1,0:T(8,128)(2,1)} custom-call(s32[2,64]{1,0:T(2,128)S(1)} %copy-done.2, bf16[2,128,4096]{2,1,0:T(8,128)(2,1)S(1)} %bitcast.3, bf16[128,1024]{1,0:T(8,128)(2,1)S(1)} %collective-permute-done.21.pk_ref.pv_ref, bf16[128,1024]{1,0:T(8,128)(2,1)S(1)} %totals.3.k_ref.v_ref, ...), custom_call_target="tpu_custom_call" | custom-call | flops 536870912 | bytes 4194304 | tf_op jit(solution)/shard_map/attend/pallas_call | solution.py:188
  132.9 4.5 %collective-permute-done.14.pk_ref.pv_ref = bf16[128,1024]{1,0:T(8,128)(2,1)S(1)} collective-permute-done((bf16[128,1024]{1,0:T(8,128)(2,1)S(1)}, bf16[128,1024]{1,0:T(8,128)(2,1)S(1)}, u32[]{:S(2)}, u32[]{:S(2)}) %collective-permute-start.14) | collective-permute-done | bytes 262176 | tf_op jit(solution)/shard_map/ppermute | solution.py:210
  137.4 3.9 %attend.3 = bf16[2,128,4096]{2,1,0:T(8,128)(2,1)} custom-call(s32[2,64]{1,0:T(2,128)S(1)} %copy-done.2, bf16[2,128,4096]{2,1,0:T(8,128)(2,1)S(1)} %bitcast.4, bf16[128,1024]{1,0:T(8,128)(2,1)S(1)} %collective-permute-done.14.pk_ref.pv_ref, bf16[128,1024]{1,0:T(8,128)(2,1)S(1)} %totals.2.k_ref.v_ref, ...), custom_call_target="tpu_custom_call", output_to_operand_aliasing={{}: (6, {})} | custom-call | flops 536870912 | bytes 4194304 | tf_op jit(solution)/shard_map/attend/pallas_call | solution.py:188
  (2 shorter events, 0.0 us)
Async XLA Ops:
  1.9 18.1 %collective-permute-start.3 = (bf16[2,256,512]{2,1,0:T(8,128)(2,1)}, bf16[2,256,512]{2,1,0:T(8,128)(2,1)S(1)}, u32[]{:S(2)}, u32[]{:S(2)}) collective-permute-start(bf16[2,256,512]{2,1,0:T(8,128)(2,1)} %pair.1.refs_4_), channel_id=1, source_target_pairs={{0,1},{1,2},{2,3},{3,4},{4,5},{5,6},{6,7},{7,0},{8,9},{9,10},{10,1... | collective-permute-start | bytes 1572872 | tf_op jit(solution)/shard_map/ppermute | solution.py:210
  3.9 16.1 %collective-permute-start.6 = (bf16[2,256,512]{2,1,0:T(8,128)(2,1)}, bf16[2,256,512]{2,1,0:T(8,128)(2,1)S(1)}, u32[]{:S(2)}, u32[]{:S(2)}) collective-permute-start(bf16[2,256,512]{2,1,0:T(8,128)(2,1)} %pair.1.refs_4_), channel_id=1, source_target_pairs={{0,7},{1,0},{2,1},{3,2},{4,3},{5,4},{6,5},{7,6},{8,15},{9,8},{10,9... | collective-permute-start | bytes 1572872 | tf_op jit(solution)/shard_map/ppermute | solution.py:210
  19.9 14.3 %collective-permute-start.4 = (bf16[2,256,512]{2,1,0:T(8,128)(2,1)S(1)}, bf16[2,256,512]{2,1,0:T(8,128)(2,1)S(1)}, u32[]{:S(2)}, u32[]{:S(2)}) collective-permute-start(bf16[2,256,512]{2,1,0:T(8,128)(2,1)S(1)} %collective-permute-done.3.refs_5_), channel_id=1, source_target_pairs={{0,1},{1,2},{2,3},{3,4},{4,5},{5,6},{6,7},{7,0},{8,9},{9,10},{10,1... | collective-permute-start | bytes 1572872 | tf_op jit(solution)/shard_map/ppermute | solution.py:210
  19.9 14.3 %collective-permute-start.7 = (bf16[2,256,512]{2,1,0:T(8,128)(2,1)S(1)}, bf16[2,256,512]{2,1,0:T(8,128)(2,1)S(1)}, u32[]{:S(2)}, u32[]{:S(2)}) collective-permute-start(bf16[2,256,512]{2,1,0:T(8,128)(2,1)S(1)} %collective-permute-done.6.refs_8_), channel_id=1, source_target_pairs={{0,7},{1,0},{2,1},{3,2},{4,3},{5,4},{6,5},{7,6},{8,15},{9,8},{10,9... | collective-permute-start | bytes 1572872 | tf_op jit(solution)/shard_map/ppermute | solution.py:210
  34.2 13.4 %collective-permute-start.5 = (bf16[2,256,512]{2,1,0:T(8,128)(2,1)S(1)}, bf16[2,256,512]{2,1,0:T(8,128)(2,1)S(1)}, u32[]{:S(2)}, u32[]{:S(2)}) collective-permute-start(bf16[2,256,512]{2,1,0:T(8,128)(2,1)S(1)} %collective-permute-done.4.refs_6_), channel_id=1, source_target_pairs={{0,1},{1,2},{2,3},{3,4},{4,5},{5,6},{6,7},{7,0},{8,9},{9,10},{10,1... | collective-permute-start | bytes 1572872 | tf_op jit(solution)/shard_map/ppermute | solution.py:210
  34.2 13.6 %collective-permute-start.8 = (bf16[2,256,512]{2,1,0:T(8,128)(2,1)S(1)}, bf16[2,256,512]{2,1,0:T(8,128)(2,1)S(1)}, u32[]{:S(2)}, u32[]{:S(2)}) collective-permute-start(bf16[2,256,512]{2,1,0:T(8,128)(2,1)S(1)} %collective-permute-done.7.refs_9_), channel_id=1, source_target_pairs={{0,7},{1,0},{2,1},{3,2},{4,3},{5,4},{6,5},{7,6},{8,15},{9,8},{10,9... | collective-permute-start | bytes 1572872 | tf_op jit(solution)/shard_map/ppermute | solution.py:210
  41.7 20.5 %collective-permute-start.15 = (bf16[128,2048]{1,0:T(8,128)(2,1)}, bf16[128,2048]{1,0:T(8,128)(2,1)S(1)}, u32[]{:S(2)}, u32[]{:S(2)}) collective-permute-start(bf16[128,2048]{1,0:T(8,128)(2,1)} %get-tuple-element.30), channel_id=1, source_target_pairs={{0,8},{8,16},{16,24},{24,0},{1,9},{9,17},{17,25},{25,1},{2,10},{10... | collective-permute-start | bytes 1572872 | tf_op jit(solution)/shard_map/ppermute | solution.py:210
  43.4 21.7 %collective-permute-start.16 = (bf16[128,2048]{1,0:T(8,128)(2,1)}, bf16[128,2048]{1,0:T(8,128)(2,1)S(1)}, u32[]{:S(2)}, u32[]{:S(2)}) collective-permute-start(bf16[128,2048]{1,0:T(8,128)(2,1)} %get-tuple-element.31), channel_id=1, source_target_pairs={{0,16},{8,24},{16,0},{24,8},{1,17},{9,25},{17,1},{25,9},{2,18},{10... | collective-permute-start | bytes 1572872 | tf_op jit(solution)/shard_map/ppermute | solution.py:210
  44.3 25.3 %collective-permute-start.17 = (bf16[128,2048]{1,0:T(8,128)(2,1)}, bf16[128,2048]{1,0:T(8,128)(2,1)S(1)}, u32[]{:S(2)}, u32[]{:S(2)}) collective-permute-start(bf16[128,2048]{1,0:T(8,128)(2,1)} %get-tuple-element.32), channel_id=1, source_target_pairs={{0,24},{8,0},{16,8},{24,16},{1,25},{9,1},{17,9},{25,17},{2,26},{10... | collective-permute-start | bytes 1572872 | tf_op jit(solution)/shard_map/ppermute | solution.py:210
  47.7 23.9 %collective-permute-start.9 = (bf16[1,256,512]{2,1,0:T(8,128)(2,1)S(1)}, bf16[1,256,512]{2,1,0:T(8,128)(2,1)S(1)}, u32[]{:S(2)}, u32[]{:S(2)}) collective-permute-start(bf16[1,256,512]{2,1,0:T(8,128)(2,1)S(1)} %slice.8), channel_id=1, source_target_pairs={{0,1},{1,2},{2,3},{3,4},{4,5},{5,6},{6,7},{7,0},{8,9},{9,10},{10,1... | collective-permute-start | bytes 786440 | tf_op jit(solution)/shard_map/ppermute | solution.py:210
  47.8 23.8 %copy-start.1 = (bf16[2,256,512]{2,1,0:T(8,128)(2,1)S(1)}, bf16[2,256,512]{2,1,0:T(8,128)(2,1)}, u32[]{:S(2)}) copy-start(bf16[2,256,512]{2,1,0:T(8,128)(2,1)} %pair.1.refs_4_) | copy-start | bytes 1572868
  47.8 23.8 %copy-start.4 = (bf16[128,2048]{1,0:T(8,128)(2,1)S(1)}, bf16[128,2048]{1,0:T(8,128)(2,1)}, u32[]{:S(2)}) copy-start(bf16[128,2048]{1,0:T(8,128)(2,1)} %get-tuple-element.29.refs_0_) | copy-start | bytes 1572868
  47.9 23.8 %collective-permute-start.10 = (bf16[1,256,512]{2,1,0:T(8,128)(2,1)S(1)}, bf16[1,256,512]{2,1,0:T(8,128)(2,1)S(1)}, u32[]{:S(2)}, u32[]{:S(2)}) collective-permute-start(bf16[1,256,512]{2,1,0:T(8,128)(2,1)S(1)} %slice.9), channel_id=1, source_target_pairs={{0,7},{1,0},{2,1},{3,2},{4,3},{5,4},{6,5},{7,6},{8,15},{9,8},{10,9... | collective-permute-start | bytes 786440 | tf_op jit(solution)/shard_map/ppermute | solution.py:210
  62.2 31.0 %collective-permute-start = (bf16[128,2048]{1,0:T(8,128)(2,1)}, bf16[128,2048]{1,0:T(8,128)(2,1)S(1)}, u32[]{:S(2)}, u32[]{:S(2)}) collective-permute-start(bf16[128,2048]{1,0:T(8,128)(2,1)} %get-tuple-element.22), channel_id=1, source_target_pairs={{0,8},{8,16},{16,24},{24,0},{1,9},{9,17},{17,25},{25,1},{2,10},{10... | collective-permute-start | bytes 1572872 | tf_op jit(solution)/shard_map/ppermute | solution.py:210
  65.1 31.0 %collective-permute-start.1 = (bf16[128,2048]{1,0:T(8,128)(2,1)}, bf16[128,2048]{1,0:T(8,128)(2,1)S(1)}, u32[]{:S(2)}, u32[]{:S(2)}) collective-permute-start(bf16[128,2048]{1,0:T(8,128)(2,1)} %get-tuple-element.23), channel_id=1, source_target_pairs={{0,16},{8,24},{16,0},{24,8},{1,17},{9,25},{17,1},{25,9},{2,18},{10... | collective-permute-start | bytes 1572872 | tf_op jit(solution)/shard_map/ppermute | solution.py:210
  69.7 26.4 %collective-permute-start.2 = (bf16[128,2048]{1,0:T(8,128)(2,1)}, bf16[128,2048]{1,0:T(8,128)(2,1)S(1)}, u32[]{:S(2)}, u32[]{:S(2)}) collective-permute-start(bf16[128,2048]{1,0:T(8,128)(2,1)} %get-tuple-element.24), channel_id=1, source_target_pairs={{0,24},{8,0},{16,8},{24,16},{1,25},{9,1},{17,9},{25,17},{2,26},{10... | collective-permute-start | bytes 1572872 | tf_op jit(solution)/shard_map/ppermute | solution.py:210
  71.7 24.4 %copy-start.3 = (bf16[128,2048]{1,0:T(8,128)(2,1)S(1)}, bf16[128,2048]{1,0:T(8,128)(2,1)}, u32[]{:S(2)}) copy-start(bf16[128,2048]{1,0:T(8,128)(2,1)} %get-tuple-element.21.refs_0_) | copy-start | bytes 1572868
  74.0 28.1 %collective-permute-start.18 = (bf16[128,1536]{1,0:T(8,128)(2,1)S(1)}, bf16[128,1536]{1,0:T(8,128)(2,1)S(1)}, u32[]{:S(2)}, u32[]{:S(2)}) collective-permute-start(bf16[128,1536]{1,0:T(8,128)(2,1)S(1)} %get-tuple-element.34), channel_id=1, source_target_pairs={{0,24},{8,0},{16,8},{24,16},{1,25},{9,1},{17,9},{25,17},{2,26},{10... | collective-permute-start | bytes 1179656 | tf_op jit(solution)/shard_map/ppermute | solution.py:210
  75.7 34.9 %collective-permute-start.19 = (bf16[128,1536]{1,0:T(8,128)(2,1)S(1)}, bf16[128,1536]{1,0:T(8,128)(2,1)S(1)}, u32[]{:S(2)}, u32[]{:S(2)}) collective-permute-start(bf16[128,1536]{1,0:T(8,128)(2,1)S(1)} %get-tuple-element.35), channel_id=1, source_target_pairs={{0,16},{8,24},{16,0},{24,8},{1,17},{9,25},{17,1},{25,9},{2,18},{10... | collective-permute-start | bytes 1179656 | tf_op jit(solution)/shard_map/ppermute | solution.py:210
  93.2 22.2 %collective-permute-start.20 = (bf16[128,1536]{1,0:T(8,128)(2,1)S(1)}, bf16[128,1536]{1,0:T(8,128)(2,1)S(1)}, u32[]{:S(2)}, u32[]{:S(2)}) collective-permute-start(bf16[128,1536]{1,0:T(8,128)(2,1)S(1)} %get-tuple-element.36), channel_id=1, source_target_pairs={{0,8},{8,16},{16,24},{24,0},{1,9},{9,17},{17,25},{25,1},{2,10},{10... | collective-permute-start | bytes 1179656 | tf_op jit(solution)/shard_map/ppermute | solution.py:210
  98.4 30.6 %copy-start = (bf16[1,2,128,4096]{3,2,1,0:T(8,128)(2,1)S(1)}, bf16[1,2,128,4096]{3,2,1,0:T(8,128)(2,1)}, u32[]{:S(2)}) copy-start(bf16[1,2,128,4096]{3,2,1,0:T(8,128)(2,1)} %param.7) | copy-start | bytes 6291460
  98.4 30.6 %copy-start.2 = (s32[2,64]{1,0:T(2,128)S(1)}, s32[2,64]{1,0:T(2,128)}, u32[]{:S(2)}) copy-start(s32[2,64]{1,0:T(2,128)} %len_ref.3) | copy-start | bytes 1540
  98.4 20.3 %collective-permute-start.11 = (bf16[128,1536]{1,0:T(8,128)(2,1)S(1)}, bf16[128,1536]{1,0:T(8,128)(2,1)S(1)}, u32[]{:S(2)}, u32[]{:S(2)}) collective-permute-start(bf16[128,1536]{1,0:T(8,128)(2,1)S(1)} %get-tuple-element.26), channel_id=1, source_target_pairs={{0,24},{8,0},{16,8},{24,16},{1,25},{9,1},{17,9},{25,17},{2,26},{10... | collective-permute-start | bytes 1179656 | tf_op jit(solution)/shard_map/ppermute | solution.py:210
  98.5 25.5 %collective-permute-start.12 = (bf16[128,1536]{1,0:T(8,128)(2,1)S(1)}, bf16[128,1536]{1,0:T(8,128)(2,1)S(1)}, u32[]{:S(2)}, u32[]{:S(2)}) collective-permute-start(bf16[128,1536]{1,0:T(8,128)(2,1)S(1)} %get-tuple-element.27), channel_id=1, source_target_pairs={{0,16},{8,24},{16,0},{24,8},{1,17},{9,25},{17,1},{25,9},{2,18},{10... | collective-permute-start | bytes 1179656 | tf_op jit(solution)/shard_map/ppermute | solution.py:210
  102.1 24.7 %collective-permute-start.13 = (bf16[128,1536]{1,0:T(8,128)(2,1)S(1)}, bf16[128,1536]{1,0:T(8,128)(2,1)S(1)}, u32[]{:S(2)}, u32[]{:S(2)}) collective-permute-start(bf16[128,1536]{1,0:T(8,128)(2,1)S(1)} %get-tuple-element.28), channel_id=1, source_target_pairs={{0,8},{8,16},{16,24},{24,0},{1,9},{9,17},{17,25},{25,1},{2,10},{10... | collective-permute-start | bytes 1179656 | tf_op jit(solution)/shard_map/ppermute | solution.py:210
  115.5 13.4 %collective-permute-start.21 = (bf16[128,1024]{1,0:T(8,128)(2,1)S(1)}, bf16[128,1024]{1,0:T(8,128)(2,1)S(1)}, u32[]{:S(2)}, u32[]{:S(2)}) collective-permute-start(bf16[128,1024]{1,0:T(8,128)(2,1)S(1)} %totals.3.k_ref.v_ref), channel_id=1, source_target_pairs={{0,1},{1,2},{2,3},{3,4},{4,5},{5,6},{6,7},{7,8},{8,9},{9,10},{10,1... | collective-permute-start | bytes 786440 | tf_op jit(solution)/shard_map/ppermute | solution.py:210
  127.0 10.4 %collective-permute-start.14 = (bf16[128,1024]{1,0:T(8,128)(2,1)S(1)}, bf16[128,1024]{1,0:T(8,128)(2,1)S(1)}, u32[]{:S(2)}, u32[]{:S(2)}) collective-permute-start(bf16[128,1024]{1,0:T(8,128)(2,1)S(1)} %totals.2.k_ref.v_ref), channel_id=1, source_target_pairs={{0,1},{1,2},{2,3},{3,4},{4,5},{5,6},{6,7},{7,8},{8,9},{9,10},{10,1... | collective-permute-start | bytes 786440 | tf_op jit(solution)/shard_map/ppermute | solution.py:210

commit v3 on v2

v3 whole, which is shorter than its diff:
```python
import functools
import math

import jax
import jax.numpy as jnp
from jax import lax
from jax.experimental import pallas as pl
from jax.experimental.pallas import tpu as pltpu
from jax.sharding import Mesh, PartitionSpec as P


HEAD = 128
Y, Z = 4, 8


def cost(flops, nbytes):
    return pl.CostEstimate(flops=flops, bytes_accessed=nbytes, transcendentals=0)


def vmem():
    return pl.BlockSpec(memory_space=pltpu.VMEM)


def hbm():
    return pl.BlockSpec(memory_space=pltpu.HBM)


CAME = [0] + [s + 1 for s in range(Z // 2 - 1)] + [-s - 1 for s in range(Z // 2 - 1)] + [Z // 2]
CHUNKS = 4
NORM_GRANT = (51200, 46592)


def norm_kernel(m, x_ref, g_ref, *refs):
    out_refs, x_buf, sem = refs[:Y], refs[Y], refs[Y + 1]
    y, z = lax.axis_index("y"), lax.axis_index("z")
    count = x_ref.shape[1] // CHUNKS
    loads = [pltpu.make_async_copy(x_ref.at[m, pl.ds(c * count, count)], x_buf.at[c], sem.at[c]) for c in range(CHUNKS)]
    for load in loads:
        load.start()
    wide = x_ref.shape[2] // (Y * Z)
    for c in range(CHUNKS):
        loads[c].wait()
        x = x_buf[c].astype(jnp.float32)
        inv = lax.rsqrt(jnp.mean(x * x, axis=-1, keepdims=True) + 1e-05)
        rows = slice(c * count, (c + 1) * count)
        for j in range(Y):
            for i in range(Z):
                at = ((y + j) & (Y - 1)) * Z + ((z - CAME[i]) & (Z - 1))
                at = pl.multiple_of(at * wide, wide)
                cols = x_buf[c, :, pl.ds(at, wide)].astype(jnp.float32)
                gain = g_ref[:, pl.ds(at, wide)].astype(jnp.float32)
                out_refs[j][rows, i * wide : (i + 1) * wide] = (cols * inv * gain).astype(jnp.bfloat16)


def norm_quarters(m, tokens, gain):
    _, count, width = tokens.shape
    return pl.pallas_call(
        functools.partial(norm_kernel, m),
        in_specs=[hbm(), vmem()],
        out_specs=[vmem()] * Y,
        out_shape=[jax.ShapeDtypeStruct((count, width // Y), jnp.bfloat16)] * Y,
        scratch_shapes=[
            pltpu.VMEM((CHUNKS, count // CHUNKS, width), jnp.bfloat16),
            pltpu.SemaphoreType.DMA((CHUNKS,)),
        ],
        cost_estimate=cost(10_000_000, 4 << 20),
        compiler_params=pltpu.CompilerParams(vmem_limit_bytes=NORM_GRANT[m] << 10),
        name="norm",
    )(tokens, gain)


def packed(ref, rows, k, v):
    wide = k.shape[1]
    high = k.astype(jnp.bfloat16)
    ref[rows, :wide] = high
    ref[rows, wide : 2 * wide] = (k - high.astype(jnp.float32)).astype(jnp.bfloat16)
    ref[rows, 2 * wide :] = v.astype(jnp.bfloat16)


def opened(ref, rows):
    wide = ref.shape[1] // 3
    k = ref[rows, :wide].astype(jnp.float32) + ref[rows, wide : 2 * wide].astype(jnp.float32)
    return k, ref[rows, 2 * wide :].astype(jnp.float32)


def product_kernel(*refs):
    a_refs, k_refs, v_refs = refs[:Y], refs[Y : Y + Z], refs[Y + Z : Y + 2 * Z]
    own_ref, keep_ref, up_ref, down_ref = refs[Y + 2 * Z :]
    count, wide = a_refs[0].shape[0], k_refs[0].shape[1]
    half = count // 2
    a = jnp.concatenate([r[...] for r in a_refs], axis=0)
    wk = jnp.concatenate([r[...] for r in k_refs], axis=0)
    wv = jnp.concatenate([r[...] for r in v_refs], axis=0)
    k = jnp.dot(a, wk, preferred_element_type=jnp.float32)
    v = jnp.dot(a, wv, preferred_element_type=jnp.float32)

    def part(j, h):
        rows = slice(j * count + h * half, j * count + (h + 1) * half)
        return k[rows], v[rows]

    top, bottom = slice(0, half), slice(half, count)
    own_ref[:, :wide], own_ref[:, wide:] = k[:count], v[:count]
    keep_ref[top, :wide], keep_ref[top, wide:] = part(3, 0)
    keep_ref[bottom, :wide], keep_ref[bottom, wide:] = part(1, 1)
    packed(up_ref, top, *part(2, 0))
    packed(up_ref, bottom, *part(3, 1))
    packed(down_ref, top, *part(1, 0))
    packed(down_ref, bottom, *part(2, 1))


def products(acts, key_rows, value_rows):
    rows, deep = acts[0].shape
    wide = key_rows[0].shape[1]
    return pl.pallas_call(
        product_kernel,
        in_specs=[vmem()] * (Y + 2 * Z),
        out_specs=[vmem()] * 4,
        out_shape=[jax.ShapeDtypeStruct((rows, 2 * wide), jnp.float32)] * 2
        + [jax.ShapeDtypeStruct((rows, 3 * wide), jnp.bfloat16)] * 2,
        cost_estimate=cost(4 * Y * rows * deep * wide, 8 << 20),
        compiler_params=pltpu.CompilerParams(vmem_limit_bytes=20 << 20),
        name="products",
    )(*acts, *key_rows, *value_rows)


def relay_kernel(keep_ref, up_ref, down_ref, on_up_ref, on_down_ref):
    half, wide = on_up_ref.shape[0], on_up_ref.shape[1] // 3
    for rows, came, on in ((slice(0, half), up_ref, on_up_ref), (slice(half, 2 * half), down_ref, on_down_ref)):
        k, v = opened(came, rows)
        packed(on, slice(0, half), k + keep_ref[rows, :wide], v + keep_ref[rows, wide:])


def relay(keep, up, down):
    half, width = up.shape[0] // 2, up.shape[1]
    return pl.pallas_call(
        relay_kernel,
        in_specs=[vmem()] * 3,
        out_specs=[vmem()] * 2,
        out_shape=[jax.ShapeDtypeStruct((half, width), jnp.bfloat16)] * 2,
        cost_estimate=cost(2_000_000, 2 << 20),
        compiler_params=pltpu.CompilerParams(vmem_limit_bytes=6 << 20),
        name="relay",
    )(keep, up, down)


def total_kernel(own_ref, up_ref, down_ref, on_up_ref, on_down_ref, out_ref):
    count, wide = own_ref.shape[0], own_ref.shape[1] // 2
    half = count // 2
    for rows, near, on in ((slice(0, half), down_ref, on_up_ref), (slice(half, count), up_ref, on_down_ref)):
        k, v = opened(near, rows)
        far_k, far_v = opened(on, slice(0, half))
        out_ref[rows, :wide] = (own_ref[rows, :wide] + k + far_k).astype(jnp.bfloat16)
        out_ref[rows, wide:] = (own_ref[rows, wide:] + v + far_v).astype(jnp.bfloat16)


def totals(own, up, down, on_up, on_down):
    return pl.pallas_call(
        total_kernel,
        in_specs=[vmem()] * 5,
        out_specs=vmem(),
        out_shape=jax.ShapeDtypeStruct(own.shape, jnp.bfloat16),
        cost_estimate=cost(2_000_000, 2 << 20),
        compiler_params=pltpu.CompilerParams(vmem_limit_bytes=6 << 20),
        name="totals",
    )(own, up, down, on_up, on_down)


def attend_kernel(slot, len_ref, q_ref, prior_ref, own_ref, *refs):
    out_ref, buf, sem = refs[-3:]
    count, width, docs = q_ref.shape[1], q_ref.shape[2], len_ref.shape[1]
    heads = own_ref.shape[1] // (2 * HEAD)
    group = width // heads
    before = lax.broadcasted_iota(jnp.int32, (docs, docs), 0) <= lax.broadcasted_iota(jnp.int32, (docs, docs), 1)
    lengths = len_ref[slot : slot + 1].astype(jnp.float32).astype(jnp.bfloat16)
    lengths = jnp.broadcast_to(lengths, (8, docs))
    ends = jnp.dot(lengths, before.astype(jnp.bfloat16), preferred_element_type=jnp.float32)[:1]
    ends = ends.astype(jnp.int32)
    base = (lax.axis_index("y") * Z + lax.axis_index("z")) * count
    position = base + lax.broadcasted_iota(jnp.int32, (count, docs), 0)
    first = jnp.max(jnp.where(ends <= position, ends, 0).astype(jnp.float32), axis=1, keepdims=True)
    first = first.astype(jnp.int32) - (base - count)
    column = lax.broadcasted_iota(jnp.int32, (count, 2 * count), 1)
    row = lax.broadcasted_iota(jnp.int32, (count, 2 * count), 0)
    allowed = (column >= first) & (column <= row + count)
    stores = []
    for h in range(heads):
        at, of = slice(h * HEAD, (h + 1) * HEAD), slice((heads + h) * HEAD, (heads + h + 1) * HEAD)
        keys = jnp.concatenate([prior_ref[:, at], own_ref[:, at]], axis=0)
        values = jnp.concatenate([prior_ref[:, of], own_ref[:, of]], axis=0)
        values = jnp.concatenate([values, jnp.ones_like(values)], axis=1)
        for g in range(group // HEAD):
            cols = slice(h * group + g * HEAD, h * group + (g + 1) * HEAD)
            s = lax.dot_general(
                q_ref[slot, :, cols], keys, (((1,), (1,)), ((), ())), preferred_element_type=jnp.float32
            )
            s = jnp.where(allowed, s, -1e30)
            e = jnp.exp2((s - jnp.max(s, axis=-1, keepdims=True)) * (HEAD**-0.5 * math.log2(math.e)))
            o = jnp.dot(e.astype(jnp.bfloat16), values, preferred_element_type=jnp.float32)
            buf[:, cols] = (o[:, :HEAD] / o[:, HEAD:]).astype(jnp.bfloat16)
        part = slice(h * group, (h + 1) * group)
        store = pltpu.make_async_copy(buf.at[:, part], out_ref.at[slot, :, part], sem.at[h])
        store.start()
        stores.append(store)
    for store in stores:
        store.wait()


def attend(slot, lengths, queries, prior, own, so_far):
    count, width = queries.shape[1], queries.shape[2]
    heads = own.shape[1] // (2 * HEAD)
    extra = [] if so_far is None else [so_far]
    return pl.pallas_call(
        functools.partial(attend_kernel, slot),
        in_specs=[vmem()] * 4 + [hbm()] * len(extra),
        out_specs=hbm(),
        out_shape=jax.ShapeDtypeStruct(queries.shape, jnp.bfloat16),
        scratch_shapes=[pltpu.VMEM((count, width), jnp.bfloat16), pltpu.SemaphoreType.DMA((heads,))],
        input_output_aliases={4: 0} if extra else {},
        cost_estimate=cost(8 * count * count * width, 4 << 20),
        compiler_params=pltpu.CompilerParams(vmem_limit_bytes=16 << 20),
        name="attend",
    )(lengths, queries, prior, own, *extra)


def hop(block, axis, count, distance, closed=True):
    return lax.ppermute(block, axis, [(i, (i + distance) % count) for i in range(count) if closed or i + distance < count])


def body(tokens, queries, gains, key_weight, value_weight, lengths):
    key_weight, value_weight = key_weight[0], value_weight[0]
    slots, _, _ = tokens.shape[1:]
    steps = Z // 2 - 1

    rows = {}
    for name, own in (("k", key_weight), ("v", value_weight)):
        rows[name, 0] = own
    for s in range(Z // 2):
        for name in "kv":
            if s < steps or name == "k":
                rows[name, s + 1] = hop(rows[name, s], "z", Z, 1)
            if s < steps or name == "v":
                rows[name, -s - 1] = hop(rows[name, -s], "z", Z, -1)
    rows["v", Z // 2] = rows["v", -(Z // 2)]
    key_rows, value_rows = ([rows[name, c] for c in CAME] for name in "kv")

    acts = []
    for m in range(slots):
        quarters = norm_quarters(m, tokens[0], gains)
        acts.append([quarters[0]] + [hop(quarters[j], "y", Y, j) for j in range(1, Y)])

    held = []
    for m in range(slots):
        own, keep, up, down = products(acts[m], key_rows, value_rows)
        up, down = hop(up, "y", Y, 1), hop(down, "y", Y, -1)
        held.append((own, keep, up, down))
    sums = []
    for m in range(slots):
        own, keep, up, down = held[m]
        on_up, on_down = relay(keep, up, down)
        on_up, on_down = hop(on_up, "y", Y, 1), hop(on_down, "y", Y, -1)
        sums.append(totals(own, up, down, on_up, on_down))
    out = None
    for m in range(slots):
        prior = hop(sums[m], ("y", "z"), Y * Z, 1, closed=False)
        out = attend(m, lengths, queries[0], prior, sums[m], out)
    return out[None]


def solution(mesh):
    split = Mesh(mesh.devices.reshape(-1, Y, Z), ("section", "y", "z"))
    spread = ("y", "z")

    return jax.shard_map(
        body,
        mesh=split,
        in_specs=(
            P("section", None, spread, None),
            P("section", None, spread, None),
            P("section", None),
            P("section", spread, None),
            P("section", spread, None),
            P(),
        ),
        out_specs=P("section", None, spread, None),
        check_vma=False,
    )
```

time: 142 us -> 112 us (0.79)
  waiting for transfers between devices: 80.9 us -> 46.5 us
  starting transfers between devices: 36.9 us -> 50.2 us
  Pallas kernels: 23.2 us -> 13.6 us
    ppermute x22 -> x30, waiting for transfers between devices: 80.9 us -> 46.5 us  [hop(): lax.ppermute(block, axis, [(i, (i + distance) % count) for i in range(cou...]
    ppermute x22 -> x30, starting transfers between devices: 36.9 us -> 50.2 us  [hop(): lax.ppermute(block, axis, [(i, (i + distance) % count) for i in range(cou...]
    pallas_call x7 -> x8, Pallas kernels: 14.7 us -> 9.78 us  [the longest x2 4.71 us: attend(): pl.pallas_call(functools.partial(attend_kernel, slot), in_specs=[vmem()]...]
    pallas_call x2, Pallas kernels: 8.5 us -> 3.8 us  [norm_quarters(): pl.pallas_call(functools.partial(norm_kernel, m), in_specs=[hbm(), vmem()...]
  transfers between devices with their start and end apart: 22 -> 30, of which waited for: 13 -> 16; matrix products, arithmetic and copies ran while one was open for 0% -> 0% of each run, Pallas kernels for 12% -> 10%
where the time goes in v3:
time: 112 us; the launch traced here: 111 us
  starting transfers between devices  50.2 us (45%)
  waiting for transfers between devices  46.5 us (42%)
  Pallas kernels  13.6 us (12%)
    ppermute x30, starting transfers between devices, hop(): lax.ppermute(block, axis, [(i, (i + distance) % count) for i in range(cou...  50.2 us
    ppermute x30, waiting for transfers between devices, hop(): lax.ppermute(block, axis, [(i, (i + distance) % count) for i in range(cou...  46.5 us
    pallas_call x2, Pallas kernels, attend(): pl.pallas_call(functools.partial(attend_kernel, slot), in_specs=[vmem()]...  4.71 us
    pallas_call x2, Pallas kernels, products(): pl.pallas_call(product_kernel, in_specs=[vmem()] * (Y + 2 * Z), out_specs...  4.66 us
    pallas_call x2, Pallas kernels, norm_quarters(): pl.pallas_call(functools.partial(norm_kernel, m), in_specs=[hbm(), vmem()...  3.8 us
  transfers between devices with their start and end apart: 30, of which 16 were waited for; matrix products, arithmetic and copies ran while one was open for 0% of the time, Pallas kernels for 10%

profile of v3, /device:TPU:8, one launch (start us, length us, event | category | flops | bytes accessed | tf_op | source)
XLA Modules:
  0.0 111.4 jit_solution(12713113137157922833)
XLA Ops:
  0.0 1.9 %collective-permute-start.3 = (bf16[256,512]{1,0:T(8,128)(2,1)}, bf16[256,512]{1,0:T(8,128)(2,1)S(1)}, u32[]{:S(2)}, u32[]{:S(2)}) collective-permute-start(bf16[256,512]{1,0:T(8,128)(2,1)} %bitcast.9), channel_id=1, source_target_pairs={{0,1},{1,2},{2,3},{3,4},{4,5},{5,6},{6,7},{7,0},{8,9},{9,10},{10,1... | collective-permute-start | bytes 786440 | tf_op jit(solution)/shard_map/ppermute | solution.py:226
  1.9 3.9 %collective-permute-start.6 = (bf16[256,512]{1,0:T(8,128)(2,1)}, bf16[256,512]{1,0:T(8,128)(2,1)S(1)}, u32[]{:S(2)}, u32[]{:S(2)}) collective-permute-start(bf16[256,512]{1,0:T(8,128)(2,1)} %bitcast.10), channel_id=1, source_target_pairs={{0,7},{1,0},{2,1},{3,2},{4,3},{5,4},{6,5},{7,6},{8,15},{9,8},{10,9... | collective-permute-start | bytes 786440 | tf_op jit(solution)/shard_map/ppermute | solution.py:226
  5.9 0.0 collective-permute-start.10
  5.9 3.2 %collective-permute-start.13 = (bf16[256,512]{1,0:T(8,128)(2,1)}, bf16[256,512]{1,0:T(8,128)(2,1)S(1)}, u32[]{:S(2)}, u32[]{:S(2)}) collective-permute-start(bf16[256,512]{1,0:T(8,128)(2,1)} %bitcast.14), channel_id=1, source_target_pairs={{0,7},{1,0},{2,1},{3,2},{4,3},{5,4},{6,5},{7,6},{8,15},{9,8},{10,9... | collective-permute-start | bytes 786440 | tf_op jit(solution)/shard_map/ppermute | solution.py:226
  9.1 4.1 %collective-permute-done.3.refs_5_ = bf16[256,512]{1,0:T(8,128)(2,1)S(1)} collective-permute-done((bf16[256,512]{1,0:T(8,128)(2,1)}, bf16[256,512]{1,0:T(8,128)(2,1)S(1)}, u32[]{:S(2)}, u32[]{:S(2)}) %collective-permute-start.3) | collective-permute-done | bytes 262176 | tf_op jit(solution)/shard_map/ppermute | solution.py:226
  13.2 3.2 %collective-permute-start.7 = (bf16[256,512]{1,0:T(8,128)(2,1)S(1)}, bf16[256,512]{1,0:T(8,128)(2,1)S(1)}, u32[]{:S(2)}, u32[]{:S(2)}) collective-permute-start(bf16[256,512]{1,0:T(8,128)(2,1)S(1)} %collective-permute-done.6.refs_8_), channel_id=1, source_target_pairs={{0,7},{1,0},{2,1},{3,2},{4,3},{5,4},{6,5},{7,6},{8,15},{9,8},{10,9... | collective-permute-start | bytes 786440 | tf_op jit(solution)/shard_map/ppermute | solution.py:226
  16.5 0.8 copy-done.2
  17.2 2.4 %norm.3 = (bf16[128,2048]{1,0:T(8,128)(2,1)S(1)}, bf16[128,2048]{1,0:T(8,128)(2,1)S(1)}, bf16[128,2048]{1,0:T(8,128)(2,1)S(1)}, bf16[128,2048]{1,0:T(8,128)(2,1)S(1)}) custom-call(bf16[2,128,8192]{2,1,0:T(8,128)(2,1)} %bitcast.5, bf16[1,8192]{1,0:T(2,128)(2,1)S(1)} %copy-done.2), custom_call_target="tpu_custom_call" | custom-call | flops 10000000 | bytes 4194304 | tf_op jit(solution)/shard_map/norm/pallas_call | solution.py:57
  19.7 1.7 %collective-permute-start.22 = (bf16[128,2048]{1,0:T(8,128)(2,1)S(1)}, bf16[128,2048]{1,0:T(8,128)(2,1)S(1)}, u32[]{:S(2)}, u32[]{:S(2)}) collective-permute-start(bf16[128,2048]{1,0:T(8,128)(2,1)S(1)} %get-tuple-element.36), channel_id=1, source_target_pairs={{0,8},{8,16},{16,24},{24,0},{1,9},{9,17},{17,25},{25,1},{2,10},{10... | collective-permute-start | bytes 1572872 | tf_op jit(solution)/shard_map/ppermute | solution.py:226
  21.3 0.0 collective-permute-done.10.refs_13_
  21.3 0.9 collective-permute-start.23
  22.3 0.0 collective-permute-done.13.refs_16_
  22.3 2.4 %collective-permute-start.24 = (bf16[128,2048]{1,0:T(8,128)(2,1)S(1)}, bf16[128,2048]{1,0:T(8,128)(2,1)S(1)}, u32[]{:S(2)}, u32[]{:S(2)}) collective-permute-start(bf16[128,2048]{1,0:T(8,128)(2,1)S(1)} %get-tuple-element.38), channel_id=1, source_target_pairs={{0,24},{8,0},{16,8},{24,16},{1,25},{9,1},{17,9},{25,17},{2,26},{10... | collective-permute-start | bytes 1572872 | tf_op jit(solution)/shard_map/ppermute | solution.py:226
  24.7 3.2 %collective-permute-start.14 = (bf16[256,512]{1,0:T(8,128)(2,1)S(1)}, bf16[256,512]{1,0:T(8,128)(2,1)S(1)}, u32[]{:S(2)}, u32[]{:S(2)}) collective-permute-start(bf16[256,512]{1,0:T(8,128)(2,1)S(1)} %collective-permute-done.13.refs_16_), channel_id=1, source_target_pairs={{0,7},{1,0},{2,1},{3,2},{4,3},{5,4},{6,5},{7,6},{8,15},{9,8},{10,9... | collective-permute-start | bytes 786440 | tf_op jit(solution)/shard_map/ppermute | solution.py:226
  27.9 4.4 %collective-permute-done.11.refs_14_ = bf16[256,512]{1,0:T(8,128)(2,1)S(1)} collective-permute-done((bf16[256,512]{1,0:T(8,128)(2,1)S(1)}, bf16[256,512]{1,0:T(8,128)(2,1)S(1)}, u32[]{:S(2)}, u32[]{:S(2)}) %collective-permute-start.11) | collective-permute-done | bytes 262176 | tf_op jit(solution)/shard_map/ppermute | solution.py:226
  32.3 3.2 %collective-permute-start.8 = (bf16[256,512]{1,0:T(8,128)(2,1)S(1)}, bf16[256,512]{1,0:T(8,128)(2,1)S(1)}, u32[]{:S(2)}, u32[]{:S(2)}) collective-permute-start(bf16[256,512]{1,0:T(8,128)(2,1)S(1)} %collective-permute-done.7.refs_9_), channel_id=1, source_target_pairs={{0,7},{1,0},{2,1},{3,2},{4,3},{5,4},{6,5},{7,6},{8,15},{9,8},{10,9... | collective-permute-start | bytes 786440 | tf_op jit(solution)/shard_map/ppermute | solution.py:226
  35.5 0.0 collective-permute-done.22.refs_1_
  35.5 0.0 collective-permute-start.12
  35.5 2.1 %collective-permute-done.23.refs_2_ = bf16[128,2048]{1,0:T(8,128)(2,1)S(1)} collective-permute-done((bf16[128,2048]{1,0:T(8,128)(2,1)S(1)}, bf16[128,2048]{1,0:T(8,128)(2,1)S(1)}, u32[]{:S(2)}, u32[]{:S(2)}) %collective-permute-start.23) | collective-permute-done | bytes 524320 | tf_op jit(solution)/shard_map/ppermute | solution.py:226
  37.6 1.2 %collective-permute-start.15 = (bf16[256,512]{1,0:T(8,128)(2,1)S(1)}, bf16[256,512]{1,0:T(8,128)(2,1)S(1)}, u32[]{:S(2)}, u32[]{:S(2)}) collective-permute-start(bf16[256,512]{1,0:T(8,128)(2,1)S(1)} %collective-permute-done.14.refs_17_), channel_id=1, source_target_pairs={{0,7},{1,0},{2,1},{3,2},{4,3},{5,4},{6,5},{7,6},{8,15},{9,8},{10,9... | collective-permute-start | bytes 786440 | tf_op jit(solution)/shard_map/ppermute | solution.py:226
  38.8 1.4 %norm.2 = (bf16[128,2048]{1,0:T(8,128)(2,1)S(1)}, bf16[128,2048]{1,0:T(8,128)(2,1)S(1)}, bf16[128,2048]{1,0:T(8,128)(2,1)S(1)}, bf16[128,2048]{1,0:T(8,128)(2,1)S(1)}) custom-call(bf16[2,128,8192]{2,1,0:T(8,128)(2,1)S(1)} %bitcast.6, bf16[1,8192]{1,0:T(2,128)(2,1)S(1)} %copy-done.3), custom_call_target="tpu_custom_call" | custom-call | flops 10000000 | bytes 4194304 | tf_op jit(solution)/shard_map/norm/pallas_call | solution.py:57
  40.2 4.6 %collective-permute-done.24.refs_3_ = bf16[128,2048]{1,0:T(8,128)(2,1)S(1)} collective-permute-done((bf16[128,2048]{1,0:T(8,128)(2,1)S(1)}, bf16[128,2048]{1,0:T(8,128)(2,1)S(1)}, u32[]{:S(2)}, u32[]{:S(2)}) %collective-permute-start.24) | collective-permute-done | bytes 524320 | tf_op jit(solution)/shard_map/ppermute | solution.py:226
  44.8 4.2 %collective-permute-start = (bf16[128,2048]{1,0:T(8,128)(2,1)S(1)}, bf16[128,2048]{1,0:T(8,128)(2,1)S(1)}, u32[]{:S(2)}, u32[]{:S(2)}) collective-permute-start(bf16[128,2048]{1,0:T(8,128)(2,1)S(1)} %get-tuple-element.26), channel_id=1, source_target_pairs={{0,8},{8,16},{16,24},{24,0},{1,9},{9,17},{17,25},{25,1},{2,10},{10... | collective-permute-start | bytes 1572872 | tf_op jit(solution)/shard_map/ppermute | solution.py:226
  48.9 0.4 collective-permute-start.1
  49.4 0.0 collective-permute-done.8.refs_10_
  49.4 1.7 %collective-permute-start.2 = (bf16[128,2048]{1,0:T(8,128)(2,1)S(1)}, bf16[128,2048]{1,0:T(8,128)(2,1)S(1)}, u32[]{:S(2)}, u32[]{:S(2)}) collective-permute-start(bf16[128,2048]{1,0:T(8,128)(2,1)S(1)} %get-tuple-element.28), channel_id=1, source_target_pairs={{0,24},{8,0},{16,8},{24,16},{1,25},{9,1},{17,9},{25,17},{2,26},{10... | collective-permute-start | bytes 1572872 | tf_op jit(solution)/shard_map/ppermute | solution.py:226
  51.1 0.0 collective-permute-done.12.refs_15_
  51.1 0.1 collective-permute-start.9
  51.2 3.1 %collective-permute-start.16 = (bf16[256,512]{1,0:T(8,128)(2,1)S(1)}, bf16[256,512]{1,0:T(8,128)(2,1)S(1)}, u32[]{:S(2)}, u32[]{:S(2)}) collective-permute-start(bf16[256,512]{1,0:T(8,128)(2,1)S(1)} %collective-permute-done.15.refs_18_), channel_id=1, source_target_pairs={{0,7},{1,0},{2,1},{3,2},{4,3},{5,4},{6,5},{7,6},{8,15},{9,8},{10,9... | collective-permute-start | bytes 786440 | tf_op jit(solution)/shard_map/ppermute | solution.py:226
  54.4 4.3 %collective-permute-done.9.refs_11_ = bf16[256,512]{1,0:T(8,128)(2,1)S(1)} collective-permute-done((bf16[256,512]{1,0:T(8,128)(2,1)S(1)}, bf16[256,512]{1,0:T(8,128)(2,1)S(1)}, u32[]{:S(2)}, u32[]{:S(2)}) %collective-permute-start.9) | collective-permute-done | bytes 262176 | tf_op jit(solution)/shard_map/ppermute | solution.py:226
  58.7 0.0 collective-permute-done.16.refs_19_
  58.7 2.3 %products.3 = (f32[128,1024]{1,0:T(8,128)S(1)}, f32[128,1024]{1,0:T(8,128)S(1)}, bf16[128,1536]{1,0:T(8,128)(2,1)S(1)}, bf16[128,1536]{1,0:T(8,128)(2,1)S(1)}) custom-call(bf16[128,2048]{1,0:T(8,128)(2,1)S(1)} %get-tuple-element.35.refs_0_, bf16[128,2048]{1,0:T(8,128)(2,1)S(1)} %collective-permute-done.22.refs_1_, ...), custom_call_target="tpu_custom_call" | custom-call | flops 2147483648 | bytes 8388608 | tf_op jit(solution)/shard_map/products/pallas_call | solution.py:114
  61.1 0.9 collective-permute-start.25
  62.0 1.8 %collective-permute-start.26 = (bf16[128,1536]{1,0:T(8,128)(2,1)S(1)}, bf16[128,1536]{1,0:T(8,128)(2,1)S(1)}, u32[]{:S(2)}, u32[]{:S(2)}) collective-permute-start(bf16[128,1536]{1,0:T(8,128)(2,1)S(1)} %get-tuple-element.41), channel_id=1, source_target_pairs={{0,24},{8,0},{16,8},{24,16},{1,25},{9,1},{17,9},{25,17},{2,26},{10... | collective-permute-start | bytes 1179656 | tf_op jit(solution)/shard_map/ppermute | solution.py:226
  63.8 0.0 collective-permute-done.refs_1_
  63.8 1.5 %collective-permute-done.1.refs_2_ = bf16[128,2048]{1,0:T(8,128)(2,1)S(1)} collective-permute-done((bf16[128,2048]{1,0:T(8,128)(2,1)S(1)}, bf16[128,2048]{1,0:T(8,128)(2,1)S(1)}, u32[]{:S(2)}, u32[]{:S(2)}) %collective-permute-start.1) | collective-permute-done | bytes 524320 | tf_op jit(solution)/shard_map/ppermute | solution.py:226
  65.2 7.7 %collective-permute-done.2.refs_3_ = bf16[128,2048]{1,0:T(8,128)(2,1)S(1)} collective-permute-done((bf16[128,2048]{1,0:T(8,128)(2,1)S(1)}, bf16[128,2048]{1,0:T(8,128)(2,1)S(1)}, u32[]{:S(2)}, u32[]{:S(2)}) %collective-permute-start.2) | collective-permute-done | bytes 524320 | tf_op jit(solution)/shard_map/ppermute | solution.py:226
  72.9 2.3 %products.2 = (f32[128,1024]{1,0:T(8,128)S(1)}, f32[128,1024]{1,0:T(8,128)S(1)}, bf16[128,1536]{1,0:T(8,128)(2,1)S(1)}, bf16[128,1536]{1,0:T(8,128)(2,1)S(1)}) custom-call(bf16[128,2048]{1,0:T(8,128)(2,1)S(1)} %get-tuple-element.25.refs_0_, bf16[128,2048]{1,0:T(8,128)(2,1)S(1)} %collective-permute-done.refs_1_, ...), custom_call_target="tpu_custom_call" | custom-call | flops 2147483648 | bytes 8388608 | tf_op jit(solution)/shard_map/products/pallas_call | solution.py:114
  75.3 2.7 %collective-permute-start.17 = (bf16[128,1536]{1,0:T(8,128)(2,1)S(1)}, bf16[128,1536]{1,0:T(8,128)(2,1)S(1)}, u32[]{:S(2)}, u32[]{:S(2)}) collective-permute-start(bf16[128,1536]{1,0:T(8,128)(2,1)S(1)} %get-tuple-element.30), channel_id=1, source_target_pairs={{0,8},{8,16},{16,24},{24,0},{1,9},{9,17},{17,25},{25,1},{2,10},{10... | collective-permute-start | bytes 1179656 | tf_op jit(solution)/shard_map/ppermute | solution.py:226
  77.9 0.0 collective-permute-start.18
  77.9 1.7 %collective-permute-done.25.up_ref = bf16[128,1536]{1,0:T(8,128)(2,1)S(1)} collective-permute-done((bf16[128,1536]{1,0:T(8,128)(2,1)S(1)}, bf16[128,1536]{1,0:T(8,128)(2,1)S(1)}, u32[]{:S(2)}, u32[]{:S(2)}) %collective-permute-start.25) | collective-permute-done | bytes 393248 | tf_op jit(solution)/shard_map/ppermute | solution.py:226
  79.6 0.7 collective-permute-done.26.down_ref
  80.3 0.1 relay.3
  80.4 0.8 collective-permute-start.27
  81.2 2.1 %collective-permute-start.28 = (bf16[64,1536]{1,0:T(8,128)(2,1)S(1)}, bf16[64,1536]{1,0:T(8,128)(2,1)S(1)}, u32[]{:S(2)}, u32[]{:S(2)}) collective-permute-start(bf16[64,1536]{1,0:T(8,128)(2,1)S(1)} %get-tuple-element.44), channel_id=1, source_target_pairs={{0,24},{8,0},{16,8},{24,16},{1,25},{9,1},{17,9},{25,17},{2,26},{10... | collective-permute-start | bytes 589832 | tf_op jit(solution)/shard_map/ppermute | solution.py:226
  83.2 4.8 %collective-permute-done.17.up_ref = bf16[128,1536]{1,0:T(8,128)(2,1)S(1)} collective-permute-done((bf16[128,1536]{1,0:T(8,128)(2,1)S(1)}, bf16[128,1536]{1,0:T(8,128)(2,1)S(1)}, u32[]{:S(2)}, u32[]{:S(2)}) %collective-permute-start.17) | collective-permute-done | bytes 393248 | tf_op jit(solution)/shard_map/ppermute | solution.py:226
  88.0 1.9 %collective-permute-done.18.down_ref = bf16[128,1536]{1,0:T(8,128)(2,1)S(1)} collective-permute-done((bf16[128,1536]{1,0:T(8,128)(2,1)S(1)}, bf16[128,1536]{1,0:T(8,128)(2,1)S(1)}, u32[]{:S(2)}, u32[]{:S(2)}) %collective-permute-start.18) | collective-permute-done | bytes 393248 | tf_op jit(solution)/shard_map/ppermute | solution.py:226
  89.9 0.1 relay.2
  90.0 0.0 copy-start.1
  90.0 0.0 copy-start.4
  90.0 0.6 collective-permute-start.19
  90.6 1.5 %collective-permute-start.20 = (bf16[64,1536]{1,0:T(8,128)(2,1)S(1)}, bf16[64,1536]{1,0:T(8,128)(2,1)S(1)}, u32[]{:S(2)}, u32[]{:S(2)}) collective-permute-start(bf16[64,1536]{1,0:T(8,128)(2,1)S(1)} %get-tuple-element.34), channel_id=1, source_target_pairs={{0,24},{8,0},{16,8},{24,16},{1,25},{9,1},{17,9},{25,17},{2,26},{10... | collective-permute-start | bytes 589832 | tf_op jit(solution)/shard_map/ppermute | solution.py:226
  92.1 0.1 collective-permute-done.27.on_up_ref
  92.2 1.6 %collective-permute-done.28.on_down_ref = bf16[64,1536]{1,0:T(8,128)(2,1)S(1)} collective-permute-done((bf16[64,1536]{1,0:T(8,128)(2,1)S(1)}, bf16[64,1536]{1,0:T(8,128)(2,1)S(1)}, u32[]{:S(2)}, u32[]{:S(2)}) %collective-permute-start.28) | collective-permute-done | bytes 196640 | tf_op jit(solution)/shard_map/ppermute | solution.py:226
  93.9 0.1 totals.3.own_ref
  94.0 2.1 %collective-permute-start.29 = (bf16[128,1024]{1,0:T(8,128)(2,1)S(1)}, bf16[128,1024]{1,0:T(8,128)(2,1)S(1)}, u32[]{:S(2)}, u32[]{:S(2)}) collective-permute-start(bf16[128,1024]{1,0:T(8,128)(2,1)S(1)} %totals.3.own_ref), channel_id=1, source_target_pairs={{0,1},{1,2},{2,3},{3,4},{4,5},{5,6},{6,7},{7,8},{8,9},{9,10},{10,1... | collective-permute-start | bytes 786440 | tf_op jit(solution)/shard_map/ppermute | solution.py:226
  96.1 0.0 collective-permute-done.19.on_up_ref
  96.1 0.7 collective-permute-done.20.on_down_ref
  96.8 0.1 totals.2.own_ref
  96.9 3.3 %collective-permute-start.21 = (bf16[128,1024]{1,0:T(8,128)(2,1)S(1)}, bf16[128,1024]{1,0:T(8,128)(2,1)S(1)}, u32[]{:S(2)}, u32[]{:S(2)}) collective-permute-start(bf16[128,1024]{1,0:T(8,128)(2,1)S(1)} %totals.2.own_ref), channel_id=1, source_target_pairs={{0,1},{1,2},{2,3},{3,4},{4,5},{5,6},{6,7},{7,8},{8,9},{9,10},{10,1... | collective-permute-start | bytes 786440 | tf_op jit(solution)/shard_map/ppermute | solution.py:226
  100.2 5.8 %collective-permute-done.29.prior_ref = bf16[128,1024]{1,0:T(8,128)(2,1)S(1)} collective-permute-done((bf16[128,1024]{1,0:T(8,128)(2,1)S(1)}, bf16[128,1024]{1,0:T(8,128)(2,1)S(1)}, u32[]{:S(2)}, u32[]{:S(2)}) %collective-permute-start.29) | collective-permute-done | bytes 262176 | tf_op jit(solution)/shard_map/ppermute | solution.py:226
  106.1 2.4 %attend.2.refs_0_ = bf16[2,128,4096]{2,1,0:T(8,128)(2,1)} custom-call(s32[2,64]{1,0:T(2,128)S(1)} %copy-done.4, bf16[2,128,4096]{2,1,0:T(8,128)(2,1)S(1)} %bitcast.7, bf16[128,1024]{1,0:T(8,128)(2,1)S(1)} %collective-permute-done.29.prior_ref, bf16[128,1024]{1,0:T(8,128)(2,1)S(1)} %totals.3.own_ref), custom_call_target="tpu_custom_call" | custom-call | flops 536870912 | bytes 4194304 | tf_op jit(solution)/shard_map/attend/pallas_call | solution.py:212
  108.4 0.4 collective-permute-done.21.prior_ref
  108.9 2.4 %attend.3 = bf16[2,128,4096]{2,1,0:T(8,128)(2,1)} custom-call(s32[2,64]{1,0:T(2,128)S(1)} %copy-done.4, bf16[2,128,4096]{2,1,0:T(8,128)(2,1)S(1)} %bitcast.8, bf16[128,1024]{1,0:T(8,128)(2,1)S(1)} %collective-permute-done.21.prior_ref, bf16[128,1024]{1,0:T(8,128)(2,1)S(1)} %totals.2.own_ref, ...), custom_call_target="tpu_custom_call", output_to_operand_aliasing={{}: (4, {})} | custom-call | flops 536870912 | bytes 4194304 | tf_op jit(solution)/shard_map/attend/pallas_call | solution.py:212
  (20 shorter events, 0.0 us)
Async XLA Ops:
  0.0 13.2 %collective-permute-start.3 = (bf16[256,512]{1,0:T(8,128)(2,1)}, bf16[256,512]{1,0:T(8,128)(2,1)S(1)}, u32[]{:S(2)}, u32[]{:S(2)}) collective-permute-start(bf16[256,512]{1,0:T(8,128)(2,1)} %bitcast.9), channel_id=1, source_target_pairs={{0,1},{1,2},{2,3},{3,4},{4,5},{5,6},{6,7},{7,0},{8,9},{9,10},{10,1... | collective-permute-start | bytes 786440 | tf_op jit(solution)/shard_map/ppermute | solution.py:226
  1.9 11.3 %collective-permute-start.6 = (bf16[256,512]{1,0:T(8,128)(2,1)}, bf16[256,512]{1,0:T(8,128)(2,1)S(1)}, u32[]{:S(2)}, u32[]{:S(2)}) collective-permute-start(bf16[256,512]{1,0:T(8,128)(2,1)} %bitcast.10), channel_id=1, source_target_pairs={{0,7},{1,0},{2,1},{3,2},{4,3},{5,4},{6,5},{7,6},{8,15},{9,8},{10,9... | collective-permute-start | bytes 786440 | tf_op jit(solution)/shard_map/ppermute | solution.py:226
  5.9 15.5 %collective-permute-start.10 = (bf16[256,512]{1,0:T(8,128)(2,1)}, bf16[256,512]{1,0:T(8,128)(2,1)S(1)}, u32[]{:S(2)}, u32[]{:S(2)}) collective-permute-start(bf16[256,512]{1,0:T(8,128)(2,1)} %bitcast.13), channel_id=1, source_target_pairs={{0,1},{1,2},{2,3},{3,4},{4,5},{5,6},{6,7},{7,0},{8,9},{9,10},{10,1... | collective-permute-start | bytes 786440 | tf_op jit(solution)/shard_map/ppermute | solution.py:226
  5.9 16.4 %collective-permute-start.13 = (bf16[256,512]{1,0:T(8,128)(2,1)}, bf16[256,512]{1,0:T(8,128)(2,1)S(1)}, u32[]{:S(2)}, u32[]{:S(2)}) collective-permute-start(bf16[256,512]{1,0:T(8,128)(2,1)} %bitcast.14), channel_id=1, source_target_pairs={{0,7},{1,0},{2,1},{3,2},{4,3},{5,4},{6,5},{7,6},{8,15},{9,8},{10,9... | collective-permute-start | bytes 786440 | tf_op jit(solution)/shard_map/ppermute | solution.py:226
  13.2 11.5 %collective-permute-start.4 = (bf16[256,512]{1,0:T(8,128)(2,1)S(1)}, bf16[256,512]{1,0:T(8,128)(2,1)S(1)}, u32[]{:S(2)}, u32[]{:S(2)}) collective-permute-start(bf16[256,512]{1,0:T(8,128)(2,1)S(1)} %collective-permute-done.3.refs_5_), channel_id=1, source_target_pairs={{0,1},{1,2},{2,3},{3,4},{4,5},{5,6},{6,7},{7,0},{8,9},{9,10},{10,1... | collective-permute-start | bytes 786440 | tf_op jit(solution)/shard_map/ppermute | solution.py:226
  13.2 11.5 %collective-permute-start.7 = (bf16[256,512]{1,0:T(8,128)(2,1)S(1)}, bf16[256,512]{1,0:T(8,128)(2,1)S(1)}, u32[]{:S(2)}, u32[]{:S(2)}) collective-permute-start(bf16[256,512]{1,0:T(8,128)(2,1)S(1)} %collective-permute-done.6.refs_8_), channel_id=1, source_target_pairs={{0,7},{1,0},{2,1},{3,2},{4,3},{5,4},{6,5},{7,6},{8,15},{9,8},{10,9... | collective-permute-start | bytes 786440 | tf_op jit(solution)/shard_map/ppermute | solution.py:226
  16.5 0.8 copy-start.2
  17.2 21.6 %copy-start = (bf16[1,2,128,8192]{3,2,1,0:T(8,128)(2,1)S(1)}, bf16[1,2,128,8192]{3,2,1,0:T(8,128)(2,1)}, u32[]{:S(2)}) copy-start(bf16[1,2,128,8192]{3,2,1,0:T(8,128)(2,1)} %param.6) | copy-start | bytes 12582916
  17.2 21.6 %copy-start.3 = (bf16[1,8192]{1,0:T(2,128)(2,1)S(1)}, bf16[1,8192]{1,0:T(2,128)(2,1)}, u32[]{:S(2)}) copy-start(bf16[1,8192]{1,0:T(2,128)(2,1)} %g_ref.3) | copy-start | bytes 49156
  19.7 15.9 %collective-permute-start.22 = (bf16[128,2048]{1,0:T(8,128)(2,1)S(1)}, bf16[128,2048]{1,0:T(8,128)(2,1)S(1)}, u32[]{:S(2)}, u32[]{:S(2)}) collective-permute-start(bf16[128,2048]{1,0:T(8,128)(2,1)S(1)} %get-tuple-element.36), channel_id=1, source_target_pairs={{0,8},{8,16},{16,24},{24,0},{1,9},{9,17},{17,25},{25,1},{2,10},{10... | collective-permute-start | bytes 1572872 | tf_op jit(solution)/shard_map/ppermute | solution.py:226
  21.3 16.3 %collective-permute-start.23 = (bf16[128,2048]{1,0:T(8,128)(2,1)S(1)}, bf16[128,2048]{1,0:T(8,128)(2,1)S(1)}, u32[]{:S(2)}, u32[]{:S(2)}) collective-permute-start(bf16[128,2048]{1,0:T(8,128)(2,1)S(1)} %get-tuple-element.37), channel_id=1, source_target_pairs={{0,16},{8,24},{16,0},{24,8},{1,17},{9,25},{17,1},{25,9},{2,18},{10... | collective-permute-start | bytes 1572872 | tf_op jit(solution)/shard_map/ppermute | solution.py:226
  22.3 36.5 %copy-start.5 = (bf16[1,256,512]{2,1,0:T(8,128)(2,1)S(1)}, bf16[1,256,512]{2,1,0:T(8,128)(2,1)}, u32[]{:S(2)}) copy-start(bf16[1,256,512]{2,1,0:T(8,128)(2,1)} %param.9) | copy-start | bytes 786436
  22.3 36.5 %copy-start.6 = (bf16[1,256,512]{2,1,0:T(8,128)(2,1)S(1)}, bf16[1,256,512]{2,1,0:T(8,128)(2,1)}, u32[]{:S(2)}) copy-start(bf16[1,256,512]{2,1,0:T(8,128)(2,1)} %param.10) | copy-start | bytes 786436
  22.3 22.5 %collective-permute-start.24 = (bf16[128,2048]{1,0:T(8,128)(2,1)S(1)}, bf16[128,2048]{1,0:T(8,128)(2,1)S(1)}, u32[]{:S(2)}, u32[]{:S(2)}) collective-permute-start(bf16[128,2048]{1,0:T(8,128)(2,1)S(1)} %get-tuple-element.38), channel_id=1, source_target_pairs={{0,24},{8,0},{16,8},{24,16},{1,25},{9,1},{17,9},{25,17},{2,26},{10... | collective-permute-start | bytes 1572872 | tf_op jit(solution)/shard_map/ppermute | solution.py:226
  24.7 7.6 %collective-permute-start.11 = (bf16[256,512]{1,0:T(8,128)(2,1)S(1)}, bf16[256,512]{1,0:T(8,128)(2,1)S(1)}, u32[]{:S(2)}, u32[]{:S(2)}) collective-permute-start(bf16[256,512]{1,0:T(8,128)(2,1)S(1)} %collective-permute-done.10.refs_13_), channel_id=1, source_target_pairs={{0,1},{1,2},{2,3},{3,4},{4,5},{5,6},{6,7},{7,0},{8,9},{9,10},{10,1... | collective-permute-start | bytes 786440 | tf_op jit(solution)/shard_map/ppermute | solution.py:226
  24.7 7.6 %collective-permute-start.14 = (bf16[256,512]{1,0:T(8,128)(2,1)S(1)}, bf16[256,512]{1,0:T(8,128)(2,1)S(1)}, u32[]{:S(2)}, u32[]{:S(2)}) collective-permute-start(bf16[256,512]{1,0:T(8,128)(2,1)S(1)} %collective-permute-done.13.refs_16_), channel_id=1, source_target_pairs={{0,7},{1,0},{2,1},{3,2},{4,3},{5,4},{6,5},{7,6},{8,15},{9,8},{10,9... | collective-permute-start | bytes 786440 | tf_op jit(solution)/shard_map/ppermute | solution.py:226
  32.3 16.7 %collective-permute-start.5 = (bf16[256,512]{1,0:T(8,128)(2,1)S(1)}, bf16[256,512]{1,0:T(8,128)(2,1)S(1)}, u32[]{:S(2)}, u32[]{:S(2)}) collective-permute-start(bf16[256,512]{1,0:T(8,128)(2,1)S(1)} %collective-permute-done.4.refs_6_), channel_id=1, source_target_pairs={{0,1},{1,2},{2,3},{3,4},{4,5},{5,6},{6,7},{7,0},{8,9},{9,10},{10,1... | collective-permute-start | bytes 786440 | tf_op jit(solution)/shard_map/ppermute | solution.py:226
  32.3 17.1 %collective-permute-start.8 = (bf16[256,512]{1,0:T(8,128)(2,1)S(1)}, bf16[256,512]{1,0:T(8,128)(2,1)S(1)}, u32[]{:S(2)}, u32[]{:S(2)}) collective-permute-start(bf16[256,512]{1,0:T(8,128)(2,1)S(1)} %collective-permute-done.7.refs_9_), channel_id=1, source_target_pairs={{0,7},{1,0},{2,1},{3,2},{4,3},{5,4},{6,5},{7,6},{8,15},{9,8},{10,9... | collective-permute-start | bytes 786440 | tf_op jit(solution)/shard_map/ppermute | solution.py:226
  35.5 15.6 %collective-permute-start.12 = (bf16[256,512]{1,0:T(8,128)(2,1)S(1)}, bf16[256,512]{1,0:T(8,128)(2,1)S(1)}, u32[]{:S(2)}, u32[]{:S(2)}) collective-permute-start(bf16[256,512]{1,0:T(8,128)(2,1)S(1)} %collective-permute-done.11.refs_14_), channel_id=1, source_target_pairs={{0,1},{1,2},{2,3},{3,4},{4,5},{5,6},{6,7},{7,0},{8,9},{9,10},{10,1... | collective-permute-start | bytes 786440 | tf_op jit(solution)/shard_map/ppermute | solution.py:226
  37.6 13.6 %collective-permute-start.15 = (bf16[256,512]{1,0:T(8,128)(2,1)S(1)}, bf16[256,512]{1,0:T(8,128)(2,1)S(1)}, u32[]{:S(2)}, u32[]{:S(2)}) collective-permute-start(bf16[256,512]{1,0:T(8,128)(2,1)S(1)} %collective-permute-done.14.refs_17_), channel_id=1, source_target_pairs={{0,7},{1,0},{2,1},{3,2},{4,3},{5,4},{6,5},{7,6},{8,15},{9,8},{10,9... | collective-permute-start | bytes 786440 | tf_op jit(solution)/shard_map/ppermute | solution.py:226
  44.8 19.0 %collective-permute-start = (bf16[128,2048]{1,0:T(8,128)(2,1)S(1)}, bf16[128,2048]{1,0:T(8,128)(2,1)S(1)}, u32[]{:S(2)}, u32[]{:S(2)}) collective-permute-start(bf16[128,2048]{1,0:T(8,128)(2,1)S(1)} %get-tuple-element.26), channel_id=1, source_target_pairs={{0,8},{8,16},{16,24},{24,0},{1,9},{9,17},{17,25},{25,1},{2,10},{10... | collective-permute-start | bytes 1572872 | tf_op jit(solution)/shard_map/ppermute | solution.py:226
  48.9 16.3 %collective-permute-start.1 = (bf16[128,2048]{1,0:T(8,128)(2,1)S(1)}, bf16[128,2048]{1,0:T(8,128)(2,1)S(1)}, u32[]{:S(2)}, u32[]{:S(2)}) collective-permute-start(bf16[128,2048]{1,0:T(8,128)(2,1)S(1)} %get-tuple-element.27), channel_id=1, source_target_pairs={{0,16},{8,24},{16,0},{24,8},{1,17},{9,25},{17,1},{25,9},{2,18},{10... | collective-permute-start | bytes 1572872 | tf_op jit(solution)/shard_map/ppermute | solution.py:226
  49.4 23.5 %collective-permute-start.2 = (bf16[128,2048]{1,0:T(8,128)(2,1)S(1)}, bf16[128,2048]{1,0:T(8,128)(2,1)S(1)}, u32[]{:S(2)}, u32[]{:S(2)}) collective-permute-start(bf16[128,2048]{1,0:T(8,128)(2,1)S(1)} %get-tuple-element.28), channel_id=1, source_target_pairs={{0,24},{8,0},{16,8},{24,16},{1,25},{9,1},{17,9},{25,17},{2,26},{10... | collective-permute-start | bytes 1572872 | tf_op jit(solution)/shard_map/ppermute | solution.py:226
  51.1 7.6 %collective-permute-start.9 = (bf16[256,512]{1,0:T(8,128)(2,1)S(1)}, bf16[256,512]{1,0:T(8,128)(2,1)S(1)}, u32[]{:S(2)}, u32[]{:S(2)}) collective-permute-start(bf16[256,512]{1,0:T(8,128)(2,1)S(1)} %collective-permute-done.5.refs_7_), channel_id=1, source_target_pairs={{0,1},{1,2},{2,3},{3,4},{4,5},{5,6},{6,7},{7,0},{8,9},{9,10},{10,1... | collective-permute-start | bytes 786440 | tf_op jit(solution)/shard_map/ppermute | solution.py:226
  51.2 7.5 %collective-permute-start.16 = (bf16[256,512]{1,0:T(8,128)(2,1)S(1)}, bf16[256,512]{1,0:T(8,128)(2,1)S(1)}, u32[]{:S(2)}, u32[]{:S(2)}) collective-permute-start(bf16[256,512]{1,0:T(8,128)(2,1)S(1)} %collective-permute-done.15.refs_18_), channel_id=1, source_target_pairs={{0,7},{1,0},{2,1},{3,2},{4,3},{5,4},{6,5},{7,6},{8,15},{9,8},{10,9... | collective-permute-start | bytes 786440 | tf_op jit(solution)/shard_map/ppermute | solution.py:226
  61.1 18.5 %collective-permute-start.25 = (bf16[128,1536]{1,0:T(8,128)(2,1)S(1)}, bf16[128,1536]{1,0:T(8,128)(2,1)S(1)}, u32[]{:S(2)}, u32[]{:S(2)}) collective-permute-start(bf16[128,1536]{1,0:T(8,128)(2,1)S(1)} %get-tuple-element.40), channel_id=1, source_target_pairs={{0,8},{8,16},{16,24},{24,0},{1,9},{9,17},{17,25},{25,1},{2,10},{10... | collective-permute-start | bytes 1179656 | tf_op jit(solution)/shard_map/ppermute | solution.py:226
  62.0 18.3 %collective-permute-start.26 = (bf16[128,1536]{1,0:T(8,128)(2,1)S(1)}, bf16[128,1536]{1,0:T(8,128)(2,1)S(1)}, u32[]{:S(2)}, u32[]{:S(2)}) collective-permute-start(bf16[128,1536]{1,0:T(8,128)(2,1)S(1)} %get-tuple-element.41), channel_id=1, source_target_pairs={{0,24},{8,0},{16,8},{24,16},{1,25},{9,1},{17,9},{25,17},{2,26},{10... | collective-permute-start | bytes 1179656 | tf_op jit(solution)/shard_map/ppermute | solution.py:226
  75.3 12.8 %collective-permute-start.17 = (bf16[128,1536]{1,0:T(8,128)(2,1)S(1)}, bf16[128,1536]{1,0:T(8,128)(2,1)S(1)}, u32[]{:S(2)}, u32[]{:S(2)}) collective-permute-start(bf16[128,1536]{1,0:T(8,128)(2,1)S(1)} %get-tuple-element.30), channel_id=1, source_target_pairs={{0,8},{8,16},{16,24},{24,0},{1,9},{9,17},{17,25},{25,1},{2,10},{10... | collective-permute-start | bytes 1179656 | tf_op jit(solution)/shard_map/ppermute | solution.py:226
  77.9 12.0 %collective-permute-start.18 = (bf16[128,1536]{1,0:T(8,128)(2,1)S(1)}, bf16[128,1536]{1,0:T(8,128)(2,1)S(1)}, u32[]{:S(2)}, u32[]{:S(2)}) collective-permute-start(bf16[128,1536]{1,0:T(8,128)(2,1)S(1)} %get-tuple-element.31), channel_id=1, source_target_pairs={{0,24},{8,0},{16,8},{24,16},{1,25},{9,1},{17,9},{25,17},{2,26},{10... | collective-permute-start | bytes 1179656 | tf_op jit(solution)/shard_map/ppermute | solution.py:226
  80.4 11.9 %collective-permute-start.27 = (bf16[64,1536]{1,0:T(8,128)(2,1)S(1)}, bf16[64,1536]{1,0:T(8,128)(2,1)S(1)}, u32[]{:S(2)}, u32[]{:S(2)}) collective-permute-start(bf16[64,1536]{1,0:T(8,128)(2,1)S(1)} %get-tuple-element.43), channel_id=1, source_target_pairs={{0,8},{8,16},{16,24},{24,0},{1,9},{9,17},{17,25},{25,1},{2,10},{10... | collective-permute-start | bytes 589832 | tf_op jit(solution)/shard_map/ppermute | solution.py:226
  81.2 12.7 %collective-permute-start.28 = (bf16[64,1536]{1,0:T(8,128)(2,1)S(1)}, bf16[64,1536]{1,0:T(8,128)(2,1)S(1)}, u32[]{:S(2)}, u32[]{:S(2)}) collective-permute-start(bf16[64,1536]{1,0:T(8,128)(2,1)S(1)} %get-tuple-element.44), channel_id=1, source_target_pairs={{0,24},{8,0},{16,8},{24,16},{1,25},{9,1},{17,9},{25,17},{2,26},{10... | collective-permute-start | bytes 589832 | tf_op jit(solution)/shard_map/ppermute | solution.py:226
  90.0 16.0 %copy-start.1 = (bf16[1,2,128,4096]{3,2,1,0:T(8,128)(2,1)S(1)}, bf16[1,2,128,4096]{3,2,1,0:T(8,128)(2,1)}, u32[]{:S(2)}) copy-start(bf16[1,2,128,4096]{3,2,1,0:T(8,128)(2,1)} %param.7) | copy-start | bytes 6291460
  90.0 16.0 %copy-start.4 = (s32[2,64]{1,0:T(2,128)S(1)}, s32[2,64]{1,0:T(2,128)}, u32[]{:S(2)}) copy-start(s32[2,64]{1,0:T(2,128)} %len_ref.3) | copy-start | bytes 1540
  90.0 6.1 %collective-permute-start.19 = (bf16[64,1536]{1,0:T(8,128)(2,1)S(1)}, bf16[64,1536]{1,0:T(8,128)(2,1)S(1)}, u32[]{:S(2)}, u32[]{:S(2)}) collective-permute-start(bf16[64,1536]{1,0:T(8,128)(2,1)S(1)} %get-tuple-element.33), channel_id=1, source_target_pairs={{0,8},{8,16},{16,24},{24,0},{1,9},{9,17},{17,25},{25,1},{2,10},{10... | collective-permute-start | bytes 589832 | tf_op jit(solution)/shard_map/ppermute | solution.py:226
  90.6 6.2 %collective-permute-start.20 = (bf16[64,1536]{1,0:T(8,128)(2,1)S(1)}, bf16[64,1536]{1,0:T(8,128)(2,1)S(1)}, u32[]{:S(2)}, u32[]{:S(2)}) collective-permute-start(bf16[64,1536]{1,0:T(8,128)(2,1)S(1)} %get-tuple-element.34), channel_id=1, source_target_pairs={{0,24},{8,0},{16,8},{24,16},{1,25},{9,1},{17,9},{25,17},{2,26},{10... | collective-permute-start | bytes 589832 | tf_op jit(solution)/shard_map/ppermute | solution.py:226
  94.0 12.1 %collective-permute-start.29 = (bf16[128,1024]{1,0:T(8,128)(2,1)S(1)}, bf16[128,1024]{1,0:T(8,128)(2,1)S(1)}, u32[]{:S(2)}, u32[]{:S(2)}) collective-permute-start(bf16[128,1024]{1,0:T(8,128)(2,1)S(1)} %totals.3.own_ref), channel_id=1, source_target_pairs={{0,1},{1,2},{2,3},{3,4},{4,5},{5,6},{6,7},{7,8},{8,9},{9,10},{10,1... | collective-permute-start | bytes 786440 | tf_op jit(solution)/shard_map/ppermute | solution.py:226
  96.9 11.9 %collective-permute-start.21 = (bf16[128,1024]{1,0:T(8,128)(2,1)S(1)}, bf16[128,1024]{1,0:T(8,128)(2,1)S(1)}, u32[]{:S(2)}, u32[]{:S(2)}) collective-permute-start(bf16[128,1024]{1,0:T(8,128)(2,1)S(1)} %totals.2.own_ref), channel_id=1, source_target_pairs={{0,1},{1,2},{2,3},{3,4},{4,5},{5,6},{6,7},{7,8},{8,9},{9,10},{10,1... | collective-permute-start | bytes 786440 | tf_op jit(solution)/shard_map/ppermute | solution.py:226
